TPU v7x, 32 devices: a whole 2x2x4 slice. The times are simulated.
32 devices in a mesh: section: 8 (over z, y), tensor: 4 (over x, core).
Axes of the slice: x: 2, y: 2, z: 4, core: 2. Of those that a mesh axis runs over, the one named last changes fastest.
Arguments:
- inputs: bfloat16 [2, 163840], P(None, 'tensor'), may hold values from -6 to 6
- cotangent: bfloat16 [2, 163840], P(None, 'tensor'), may hold values from -6 to 6
- weights: bfloat16 [8, 2560, 10240], P('section', None, 'tensor'), may hold values from -0.0625 to 0.0625
- norm_gains: float32 [4, 2560], replicated, may hold values from 0.5 to 1.5
Outputs:
- layer_results: bfloat16 [8, 2, 163840], P('section', None, 'tensor')
All inputs are finite; a program needn't handle non-finite values.
Results may differ from a plain program's by a relative error of at most 0.02.
Values may be sent and summed in bfloat16 or wider, within the bound.
No kernel may reach another device: no remote copies, remote signals or barrier semaphores. Data moves between devices by JAX's collectives and lax.ppermute only.
A program may use at most 64 MiB of HBM per device.

v0:
```python
import functools

import jax
import jax.numpy as jnp
from jax import lax
from jax.experimental import pallas as pl
from jax.experimental.pallas import tpu as pltpu
from jax.sharding import PartitionSpec as P

LAYERS = 4
epsilon = 1e-05
AXES = ("section", "tensor")
f32, bf16 = jnp.float32, jnp.bfloat16
VMEM = pl.BlockSpec(memory_space=pltpu.VMEM)
SMEM = pl.BlockSpec(memory_space=pltpu.SMEM)
HBM = pl.BlockSpec(memory_space=pl.ANY)


def params(mib=8):
    return pltpu.CompilerParams(vmem_limit_bytes=mib * 1024 * 1024)


def tile_of(width):
    for tile in (512, 256, 128):
        if width % tile == 0:
            return tile
    return width


def gelu_both(v):
    c = 0.7978845608028654
    v2 = v * v
    th = jnp.tanh(c * v * (1.0 + 0.044715 * v2))
    half = 0.5 * (1.0 + th)
    slope = half + 0.5 * v * (1.0 - th * th) * (c * (1.0 + 3 * 0.044715 * v2))
    return v * half, slope


def inverse_rms_of(rows):
    return lax.rsqrt(jnp.mean(rows * rows, axis=-1, keepdims=True) + epsilon)


def load_weights(w):
    def kernel(src, dst, sem):
        copy = pltpu.make_async_copy(src, dst, sem)
        copy.start()
        copy.wait()

    return pl.pallas_call(
        kernel,
        in_specs=[HBM],
        out_specs=VMEM,
        out_shape=pltpu.VMEM(w.shape, w.dtype),
        scratch_shapes=[pltpu.SemaphoreType.DMA(())],
        compiler_params=params(16),
        name="load_weights",
    )(w)


def first_kernel(mode, tile, *refs):
    if mode == "fwd":
        part, got, gain, w, out, slope, a = refs
        up = None
    elif mode == "bwd":
        part, got, w, out, a = refs
    else:
        flag, part, got, gain, w, out, slope, a = refs
        up = flag[0] == 1
    h = part.shape[0]
    for i, ref in enumerate((part, got)):
        if mode == "bwd":
            a[i * h:(i + 1) * h] = ref[...]
        else:
            x = ref[...].astype(f32)
            n = (x * inverse_rms_of(x) * gain[...]).astype(bf16)
            if up is not None:
                n = jnp.where(up, n, ref[...])
            a[i * h:(i + 1) * h] = n

    def step(i, carry):
        at = pl.ds(pl.multiple_of(i * tile, tile), tile)
        y = jnp.dot(a[...], w[:, at], preferred_element_type=f32)
        if mode == "bwd":
            out[:, at] = y.astype(bf16)
        else:
            value, grad = gelu_both(y)
            slope[:, at] = grad.astype(bf16)
            if up is not None:
                value = jnp.where(up, value, y)
            out[:, at] = value.astype(bf16)
        return carry

    lax.fori_loop(0, w.shape[1] // tile, step, 0)


def first(mode, flag, part, got, gain, w):
    rows = 2 * part.shape[0]
    D, F = w.shape
    shape = jax.ShapeDtypeStruct((rows, F), bf16)
    args = {"fwd": (part, got, gain, w), "bwd": (part, got, w)}.get(
        mode, (flag, part, got, gain, w)
    )
    specs = [VMEM] * len(args)
    if mode == "mix":
        specs[0] = SMEM
    count = 1 if mode == "bwd" else 2
    return pl.pallas_call(
        functools.partial(first_kernel, mode, tile_of(F)),
        in_specs=specs,
        out_specs=[VMEM] * count,
        out_shape=[shape] * count,
        scratch_shapes=[pltpu.VMEM((rows, D), bf16)],
        compiler_params=params(),
        cost_estimate=pl.CostEstimate(
            flops=2 * rows * D * F, bytes_accessed=2 * D * F, transcendentals=rows * F
        ),
        name="first_" + mode,
    )(*args)


def second_kernel(mode, tile, *refs):
    if mode == "fwd":
        arrived, w, keep, give, a = refs
        src = arrived
    elif mode == "bwd":
        arrived, slope, w, keep, give, a = refs
    else:
        flag, arrived, slope, w, keep, give, a = refs
    if mode == "fwd":
        a = arrived
    else:
        z = arrived[...]
        d = (z.astype(f32) * slope[...].astype(f32)).astype(bf16)
        if mode == "mix":
            d = jnp.where(flag[0] == 1, d, z)
        a[...] = d
    h = keep.shape[0]

    def step(i, carry):
        at = pl.ds(pl.multiple_of(i * tile, tile), tile)
        y = lax.dot_general(
            a[...], w[at, :], (((1,), (1,)), ((), ())), preferred_element_type=f32
        )
        keep[:, at] = y[:h]
        give[:, at] = y[h:].astype(bf16)
        return carry

    lax.fori_loop(0, w.shape[0] // tile, step, 0)


def second(mode, flag, arrived, slope, w):
    rows, F = arrived.shape
    D = w.shape[0]
    args = {"fwd": (arrived, w), "bwd": (arrived, slope, w)}.get(
        mode, (flag, arrived, slope, w)
    )
    specs = [VMEM] * len(args)
    if mode == "mix":
        specs[0] = SMEM
    return pl.pallas_call(
        functools.partial(second_kernel, mode, tile_of(D)),
        in_specs=specs,
        out_specs=[VMEM] * 2,
        out_shape=[
            jax.ShapeDtypeStruct((rows // 2, D), f32),
            jax.ShapeDtypeStruct((rows // 2, D), bf16),
        ],
        scratch_shapes=[pltpu.VMEM((rows, F), bf16)],
        compiler_params=params(),
        cost_estimate=pl.CostEstimate(
            flops=2 * rows * D * F, bytes_accessed=2 * D * F, transcendentals=0
        ),
        name="second_" + mode,
    )(*args)


def finish_kernel(mode, *refs):
    if mode == "fwd":
        total, got, rest, out = refs
        out[...] = (
            rest[...].astype(f32) + (total[...].astype(f32) + got[...].astype(f32))
        ).astype(bf16)
        return
    if mode == "bwd":
        total, got, rest, saved, gain, out = refs
    else:
        flag, total, got, rest, saved, gain, out = refs
    summed = total[...].astype(f32) + got[...].astype(f32)
    x = saved[...].astype(f32)
    scale = inverse_rms_of(x)
    unit = x * scale
    gu = summed * gain[...]
    delta = scale * (gu - unit * jnp.mean(gu * unit, axis=-1, keepdims=True))
    if mode == "mix":
        delta = jnp.where(flag[0] == 1, delta, summed)
    out[...] = (rest[...].astype(f32) + delta).astype(bf16)


def finish(mode, flag, total, got, rest, saved, gain):
    args = {
        "fwd": (total, got, rest),
        "bwd": (total, got, rest, saved, gain),
    }.get(mode, (flag, total, got, rest, saved, gain))
    specs = [VMEM] * len(args)
    if mode == "mix":
        specs[0] = SMEM
    return pl.pallas_call(
        functools.partial(finish_kernel, mode),
        in_specs=specs,
        out_specs=VMEM,
        out_shape=jax.ShapeDtypeStruct(rest.shape, bf16),
        compiler_params=params(),
        name="finish_" + mode,
    )(*args)


def body(inputs, cotangent, weights, norm_gains):
    S = lax.axis_size("section")
    T = lax.axis_size("tensor")
    stacks = S // (2 * LAYERS)
    stride = 2 * stacks
    si = lax.axis_index("section")
    ti = lax.axis_index("tensor")
    group = si % stride // 2
    layer = si // stride
    up = si % 2 == 0
    D = weights.shape[1]
    B = inputs.shape[0] // stacks
    share = inputs.shape[1] // D
    hi = T // 2
    h = hi * share
    top = 2 * (LAYERS - 1)
    bits = T.bit_length() - 1

    def send(x, pairs, flip=0):
        route = [(a * T + t, b * T + (t ^ flip)) for a, b in pairs for t in range(T)]
        return lax.ppermute(x, AXES, route)

    def section(k, q, down):
        return k * stride + 2 * q + down

    def each(pairs):
        return [(section(a, q, i), section(b, q, j)) for a, i, b, j in pairs for q in range(stacks)]

    gain = lax.dynamic_index_in_dim(norm_gains, group * LAYERS + layer, 0, keepdims=True)
    flag = jnp.where(up, 1, 0).astype(jnp.int32).reshape(1)
    own_in = lax.dynamic_slice_in_dim(inputs, group * B, B, 0).reshape(B, share, D)
    own_cot = lax.dynamic_slice_in_dim(cotangent, group * B, B, 0).reshape(B, share, D)

    def spread(x, users):
        x = x[None]
        for bit in range(1, bits):
            got = send(x, users, 1 << bit)
            high = (ti >> bit) % 2 == 1
            x = jnp.where(
                high, jnp.concatenate([got, x], 0), jnp.concatenate([x, got], 0)
            )
        return x.reshape(h, D)

    low_users = each([(0, 0, 0, 0), (0, 1, 0, 1)])
    high_users = each([(LAYERS - 1, 0, LAYERS - 1, 0), (LAYERS - 1, 1, LAYERS - 1, 1)])
    first_layer = layer == 0
    users = low_users + high_users
    seed = [
        spread(jnp.where(first_layer, own_in[b], own_cot[b]), users) for b in range(B)
    ]
    w = load_weights(weights[0])
    main = list(seed)
    rest = list(seed)
    saved = [[None] * LAYERS for _ in range(B)]
    slopes = [[None] * LAYERS for _ in range(B)]
    results = [jnp.zeros((share, D), bf16) for _ in range(B)]
    last = layer == LAYERS - 1

    for t in range(top + 1):
        forward = t < LAYERS
        backward = t >= LAYERS - 1
        mode = "mix" if forward and backward else ("fwd" if forward else "bwd")
        k, j = t, top - t
        swap, here, cross, along = [], [], [], []
        if forward:
            swap.append((k, 0, k, 1))
            here.append((k, 1, k, 1))
            if k + 1 < LAYERS:
                cross.append((k, 1, k + 1, 0))
                along.append((k, 1, k + 1, 1))
        if backward:
            swap.append((j, 1, j, 0))
            here.append((j, 0, j, 0))
            if j > 0:
                cross.append((j, 0, j - 1, 1))
                along.append((j, 0, j - 1, 0))
        joined = ([(k, 0, k, 0)] if forward else []) + ([(j, 1, j, 1)] if backward else [])
        swap, here, cross, along, joined = map(each, (swap, here, cross, along, joined))
        if t == LAYERS - 1:
            main = [jnp.where(last & ~up, seed[b], main[b]) for b in range(B)]
            rest = [jnp.where(last & up, seed[b], rest[b]) for b in range(B)]
        arrived = []
        for b in range(B):
            got = send(main[b], joined, 1)
            if forward:
                saved[b][k] = main[b]
                out, slopes[b][k] = first(mode, flag, main[b], got, gain, w)
            else:
                (out,) = first(mode, flag, main[b], got, gain, w)
            arrived.append(send(out, swap))
        fresh = []
        for b in range(B):
            keep, give = second(
                mode, flag, arrived[b], slopes[b][j] if backward else None, w
            )
            total = keep + send(give, here, 1).astype(f32)
            for bit in range(1, bits):
                mine = total.astype(bf16)
                got = send(mine, here, 1 << bit)
                if bit < bits - 1:
                    total = mine.astype(f32) + got.astype(f32)
            fresh.append(
                finish(mode, flag, mine, got, rest[b], saved[b][j] if backward else None, gain)
            )
        ok = jnp.zeros((), bool)
        if forward:
            ok = ok | (~up & (layer == k))
        if backward:
            ok = ok | (up & (layer == j))
        for b in range(B):
            mine = lax.dynamic_index_in_dim(
                fresh[b].reshape(hi, share, D), ti // 2, 0, keepdims=False
            )
            results[b] = jnp.where(ok, mine, results[b])
        if t < top:
            main = [send(fresh[b], cross) for b in range(B)]
            rest = [send(fresh[b], along) for b in range(B)]
            if t + 1 < LAYERS - 1:
                pass
    return jnp.stack(results).reshape(1, B, share * D)


def solution(mesh):
    placed = (P(None, "tensor"), P(None, "tensor"), P("section", None, "tensor"), P())
    return jax.shard_map(
        body, mesh=mesh, in_specs=placed, out_specs=P("section", None, "tensor"), check_vma=False
    )
```

profile of v0, /device:TPU:0, one launch (start us, length us, event | category | flops | bytes accessed | tf_op | source)
XLA Modules:
  0.0 489.1 jit_solution(11042467936820552000)
XLA Ops:
  2.4 8.4 %collective-permute-start = (bf16[1,16,2560]{2,1,0:T(8,128)(2,1)S(1)}, bf16[1,16,2560]{2,1,0:T(8,128)(2,1)S(1)}, u32[]{:S(2)}, u32[]{:S(2)}) collective-permute-start(bf16[1,16,2560]{2,1,0:T(8,128)(2,1)S(1)} %select_n.232), channel_id=1, source_target_pairs={{0,2},{1,3},{2,0},{3,1},{4,6},{5,7},{6,4},{7,5},{24,26},{25,27},{2... | collective-permute-start | bytes 245768 | tf_op jit(solution)/shard_map/ppermute | solution.py:237
  10.9 7.0 %collective-permute-start.41 = (bf16[1,16,2560]{2,1,0:T(8,128)(2,1)S(1)}, bf16[1,16,2560]{2,1,0:T(8,128)(2,1)S(1)}, u32[]{:S(2)}, u32[]{:S(2)}) collective-permute-start(bf16[1,16,2560]{2,1,0:T(8,128)(2,1)S(1)} %select_n.256), channel_id=1, source_target_pairs={{0,2},{1,3},{2,0},{3,1},{4,6},{5,7},{6,4},{7,5},{24,26},{25,27},{2... | collective-permute-start | bytes 245768 | tf_op jit(solution)/shard_map/ppermute | solution.py:237
  78.1 32.3 %collective-permute-start.9 = (bf16[32,2560]{1,0:T(8,128)(2,1)S(1)}, bf16[32,2560]{1,0:T(8,128)(2,1)S(1)}, u32[]{:S(2)}, u32[]{:S(2)}) collective-permute-start(bf16[32,2560]{1,0:T(8,128)(2,1)S(1)} %add_convert_fusion.12.refs_0_), channel_id=1, source_target_pairs={{12,14},{13,15},{14,12},{15,13}} | collective-permute-start | bytes 491528 | tf_op jit(solution)/shard_map/ppermute | solution.py:237
  110.4 6.4 %collective-permute-start.50 = (bf16[32,2560]{1,0:T(8,128)(2,1)S(1)}, bf16[32,2560]{1,0:T(8,128)(2,1)S(1)}, u32[]{:S(2)}, u32[]{:S(2)}) collective-permute-start(bf16[32,2560]{1,0:T(8,128)(2,1)S(1)} %add_convert_fusion.5.refs_0_), channel_id=1, source_target_pairs={{12,14},{13,15},{14,12},{15,13}} | collective-permute-start | bytes 491528 | tf_op jit(solution)/shard_map/ppermute | solution.py:237
  116.9 6.4 %collective-permute-start.11 = (bf16[32,2560]{1,0:T(8,128)(2,1)S(1)}, bf16[32,2560]{1,0:T(8,128)(2,1)S(1)}, u32[]{:S(2)}, u32[]{:S(2)}) collective-permute-start(bf16[32,2560]{1,0:T(8,128)(2,1)S(1)} %finish_fwd.7), channel_id=1, source_target_pairs={{12,16},{13,17},{14,18},{15,19}} | collective-permute-start | bytes 491528 | tf_op jit(solution)/shard_map/ppermute | solution.py:237
  123.4 6.4 %collective-permute-start.52 = (bf16[32,2560]{1,0:T(8,128)(2,1)S(1)}, bf16[32,2560]{1,0:T(8,128)(2,1)S(1)}, u32[]{:S(2)}, u32[]{:S(2)}) collective-permute-start(bf16[32,2560]{1,0:T(8,128)(2,1)S(1)} %finish_fwd.10), channel_id=1, source_target_pairs={{12,16},{13,17},{14,18},{15,19}} | collective-permute-start | bytes 491528 | tf_op jit(solution)/shard_map/ppermute | solution.py:237
  134.6 11.7 %collective-permute-start.13 = (bf16[64,2560]{1,0:T(8,128)(2,1)S(1)}, bf16[64,2560]{1,0:T(8,128)(2,1)S(1)}, u32[]{:S(2)}, u32[]{:S(2)}) collective-permute-start(bf16[64,2560]{1,0:T(8,128)(2,1)S(1)} %get-tuple-element.55), channel_id=1, source_target_pairs={{16,20},{17,21},{18,22},{19,23}} | collective-permute-start | bytes 983048 | tf_op jit(solution)/shard_map/ppermute | solution.py:237
  150.4 6.4 %collective-permute-start.54 = (bf16[64,2560]{1,0:T(8,128)(2,1)S(1)}, bf16[64,2560]{1,0:T(8,128)(2,1)S(1)}, u32[]{:S(2)}, u32[]{:S(2)}) collective-permute-start(bf16[64,2560]{1,0:T(8,128)(2,1)S(1)} %get-tuple-element.77), channel_id=1, source_target_pairs={{16,20},{17,21},{18,22},{19,23}} | collective-permute-start | bytes 983048 | tf_op jit(solution)/shard_map/ppermute | solution.py:237
  162.0 6.7 %collective-permute-start.16 = (bf16[32,2560]{1,0:T(8,128)(2,1)S(1)}, bf16[32,2560]{1,0:T(8,128)(2,1)S(1)}, u32[]{:S(2)}, u32[]{:S(2)}) collective-permute-start(bf16[32,2560]{1,0:T(8,128)(2,1)S(1)} %finish_fwd.7), channel_id=1, source_target_pairs={{12,20},{13,21},{14,22},{15,23}} | collective-permute-start | bytes 491528 | tf_op jit(solution)/shard_map/ppermute | solution.py:237
  168.7 6.4 %collective-permute-start.57 = (bf16[32,2560]{1,0:T(8,128)(2,1)S(1)}, bf16[32,2560]{1,0:T(8,128)(2,1)S(1)}, u32[]{:S(2)}, u32[]{:S(2)}) collective-permute-start(bf16[32,2560]{1,0:T(8,128)(2,1)S(1)} %finish_fwd.10), channel_id=1, source_target_pairs={{12,20},{13,21},{14,22},{15,23}} | collective-permute-start | bytes 491528 | tf_op jit(solution)/shard_map/ppermute | solution.py:237
  180.4 6.7 %collective-permute-start.15 = (bf16[32,2560]{1,0:T(8,128)(2,1)S(1)}, bf16[32,2560]{1,0:T(8,128)(2,1)S(1)}, u32[]{:S(2)}, u32[]{:S(2)}) collective-permute-start(bf16[32,2560]{1,0:T(8,128)(2,1)S(1)} %add_convert_fusion.11.refs_0_), channel_id=1, source_target_pairs={{20,22},{21,23},{22,20},{23,21}} | collective-permute-start | bytes 491528 | tf_op jit(solution)/shard_map/ppermute | solution.py:237
  187.2 6.4 %collective-permute-start.56 = (bf16[32,2560]{1,0:T(8,128)(2,1)S(1)}, bf16[32,2560]{1,0:T(8,128)(2,1)S(1)}, u32[]{:S(2)}, u32[]{:S(2)}) collective-permute-start(bf16[32,2560]{1,0:T(8,128)(2,1)S(1)} %add_convert_fusion.4.refs_0_), channel_id=1, source_target_pairs={{20,22},{21,23},{22,20},{23,21}} | collective-permute-start | bytes 491528 | tf_op jit(solution)/shard_map/ppermute | solution.py:237
  193.7 6.4 %collective-permute-start.17 = (bf16[32,2560]{1,0:T(8,128)(2,1)S(1)}, bf16[32,2560]{1,0:T(8,128)(2,1)S(1)}, u32[]{:S(2)}, u32[]{:S(2)}) collective-permute-start(bf16[32,2560]{1,0:T(8,128)(2,1)S(1)} %finish_fwd.8), channel_id=1, source_target_pairs={{20,24},{21,25},{22,26},{23,27}} | collective-permute-start | bytes 491528 | tf_op jit(solution)/shard_map/ppermute | solution.py:237
  200.1 6.4 %collective-permute-start.22 = (bf16[32,2560]{1,0:T(8,128)(2,1)S(1)}, bf16[32,2560]{1,0:T(8,128)(2,1)S(1)}, u32[]{:S(2)}, u32[]{:S(2)}) collective-permute-start(bf16[32,2560]{1,0:T(8,128)(2,1)S(1)} %finish_fwd.8), channel_id=1, source_target_pairs={{20,28},{21,29},{22,30},{23,31}} | collective-permute-start | bytes 491528 | tf_op jit(solution)/shard_map/ppermute | solution.py:237
  212.9 6.4 %collective-permute-start.63 = (bf16[32,2560]{1,0:T(8,128)(2,1)S(1)}, bf16[32,2560]{1,0:T(8,128)(2,1)S(1)}, u32[]{:S(2)}, u32[]{:S(2)}) collective-permute-start(bf16[32,2560]{1,0:T(8,128)(2,1)S(1)} %finish_fwd.11), channel_id=1, source_target_pairs={{20,28},{21,29},{22,30},{23,31}} | collective-permute-start | bytes 491528 | tf_op jit(solution)/shard_map/ppermute | solution.py:237
  229.0 12.7 %collective-permute-start.19 = (bf16[64,2560]{1,0:T(8,128)(2,1)S(1)}, bf16[64,2560]{1,0:T(8,128)(2,1)S(1)}, u32[]{:S(2)}, u32[]{:S(2)}) collective-permute-start(bf16[64,2560]{1,0:T(8,128)(2,1)S(1)} %get-tuple-element.58), channel_id=1, source_target_pairs={{24,28},{25,29},{26,30},{27,31},{28,24},{29,25},{30,26},{31,27}} | collective-permute-start | bytes 983048 | tf_op jit(solution)/shard_map/ppermute | solution.py:237
  245.2 7.0 %collective-permute-start.60 = (bf16[64,2560]{1,0:T(8,128)(2,1)S(1)}, bf16[64,2560]{1,0:T(8,128)(2,1)S(1)}, u32[]{:S(2)}, u32[]{:S(2)}) collective-permute-start(bf16[64,2560]{1,0:T(8,128)(2,1)S(1)} %get-tuple-element.80), channel_id=1, source_target_pairs={{24,28},{25,29},{26,30},{27,31},{28,24},{29,25},{30,26},{31,27}} | collective-permute-start | bytes 983048 | tf_op jit(solution)/shard_map/ppermute | solution.py:237
  263.0 11.5 %collective-permute-start.21 = (bf16[32,2560]{1,0:T(8,128)(2,1)S(1)}, bf16[32,2560]{1,0:T(8,128)(2,1)S(1)}, u32[]{:S(2)}, u32[]{:S(2)}) collective-permute-start(bf16[32,2560]{1,0:T(8,128)(2,1)S(1)} %add_convert_fusion.10.refs_1_), channel_id=1, source_target_pairs={{28,30},{29,31},{30,28},{31,29},{24,26},{25,27},{26,24},{27,25}} | collective-permute-start | bytes 491528 | tf_op jit(solution)/shard_map/ppermute | solution.py:237
  274.6 7.0 %collective-permute-start.62 = (bf16[32,2560]{1,0:T(8,128)(2,1)S(1)}, bf16[32,2560]{1,0:T(8,128)(2,1)S(1)}, u32[]{:S(2)}, u32[]{:S(2)}) collective-permute-start(bf16[32,2560]{1,0:T(8,128)(2,1)S(1)} %add_convert_fusion.3.refs_1_), channel_id=1, source_target_pairs={{28,30},{29,31},{30,28},{31,29},{24,26},{25,27},{26,24},{27,25}} | collective-permute-start | bytes 491528 | tf_op jit(solution)/shard_map/ppermute | solution.py:237
  281.9 7.0 %collective-permute-start.23 = (bf16[32,2560]{1,0:T(8,128)(2,1)S(1)}, bf16[32,2560]{1,0:T(8,128)(2,1)S(1)}, u32[]{:S(2)}, u32[]{:S(2)}) collective-permute-start(bf16[32,2560]{1,0:T(8,128)(2,1)S(1)} %finish_mix.2), channel_id=1, source_target_pairs={{24,20},{25,21},{26,22},{27,23}} | collective-permute-start | bytes 491528 | tf_op jit(solution)/shard_map/ppermute | solution.py:237
  289.3 6.5 %collective-permute-start.64 = (bf16[32,2560]{1,0:T(8,128)(2,1)S(1)}, bf16[32,2560]{1,0:T(8,128)(2,1)S(1)}, u32[]{:S(2)}, u32[]{:S(2)}) collective-permute-start(bf16[32,2560]{1,0:T(8,128)(2,1)S(1)} %finish_mix.3), channel_id=1, source_target_pairs={{24,20},{25,21},{26,22},{27,23}} | collective-permute-start | bytes 491528 | tf_op jit(solution)/shard_map/ppermute | solution.py:237
  300.1 12.8 %collective-permute-start.25 = (bf16[64,2560]{1,0:T(8,128)(2,1)S(1)}, bf16[64,2560]{1,0:T(8,128)(2,1)S(1)}, u32[]{:S(2)}, u32[]{:S(2)}) collective-permute-start(bf16[64,2560]{1,0:T(8,128)(2,1)S(1)} %first_bwd.6), channel_id=1, source_target_pairs={{20,16},{21,17},{22,18},{23,19}} | collective-permute-start | bytes 983048 | tf_op jit(solution)/shard_map/ppermute | solution.py:237
  315.8 6.4 %collective-permute-start.66 = (bf16[64,2560]{1,0:T(8,128)(2,1)S(1)}, bf16[64,2560]{1,0:T(8,128)(2,1)S(1)}, u32[]{:S(2)}, u32[]{:S(2)}) collective-permute-start(bf16[64,2560]{1,0:T(8,128)(2,1)S(1)} %first_bwd.9), channel_id=1, source_target_pairs={{20,16},{21,17},{22,18},{23,19}} | collective-permute-start | bytes 983048 | tf_op jit(solution)/shard_map/ppermute | solution.py:237
  327.6 6.6 %collective-permute-start.28 = (bf16[32,2560]{1,0:T(8,128)(2,1)S(1)}, bf16[32,2560]{1,0:T(8,128)(2,1)S(1)}, u32[]{:S(2)}, u32[]{:S(2)}) collective-permute-start(bf16[32,2560]{1,0:T(8,128)(2,1)S(1)} %finish_mix.2), channel_id=1, source_target_pairs={{24,16},{25,17},{26,18},{27,19}} | collective-permute-start | bytes 491528 | tf_op jit(solution)/shard_map/ppermute | solution.py:237
  334.2 6.4 %collective-permute-start.69 = (bf16[32,2560]{1,0:T(8,128)(2,1)S(1)}, bf16[32,2560]{1,0:T(8,128)(2,1)S(1)}, u32[]{:S(2)}, u32[]{:S(2)}) collective-permute-start(bf16[32,2560]{1,0:T(8,128)(2,1)S(1)} %finish_mix.3), channel_id=1, source_target_pairs={{24,16},{25,17},{26,18},{27,19}} | collective-permute-start | bytes 491528 | tf_op jit(solution)/shard_map/ppermute | solution.py:237
  346.0 6.4 %collective-permute-start.27 = (bf16[32,2560]{1,0:T(8,128)(2,1)S(1)}, bf16[32,2560]{1,0:T(8,128)(2,1)S(1)}, u32[]{:S(2)}, u32[]{:S(2)}) collective-permute-start(bf16[32,2560]{1,0:T(8,128)(2,1)S(1)} %add_convert_fusion.9.refs_0_), channel_id=1, source_target_pairs={{16,18},{17,19},{18,16},{19,17}} | collective-permute-start | bytes 491528 | tf_op jit(solution)/shard_map/ppermute | solution.py:237
  352.4 6.4 %collective-permute-start.68 = (bf16[32,2560]{1,0:T(8,128)(2,1)S(1)}, bf16[32,2560]{1,0:T(8,128)(2,1)S(1)}, u32[]{:S(2)}, u32[]{:S(2)}) collective-permute-start(bf16[32,2560]{1,0:T(8,128)(2,1)S(1)} %add_convert_fusion.2.refs_0_), channel_id=1, source_target_pairs={{16,18},{17,19},{18,16},{19,17}} | collective-permute-start | bytes 491528 | tf_op jit(solution)/shard_map/ppermute | solution.py:237
  359.2 6.4 %collective-permute-start.29 = (bf16[32,2560]{1,0:T(8,128)(2,1)S(1)}, bf16[32,2560]{1,0:T(8,128)(2,1)S(1)}, u32[]{:S(2)}, u32[]{:S(2)}) collective-permute-start(bf16[32,2560]{1,0:T(8,128)(2,1)S(1)} %finish_bwd.6), channel_id=1, source_target_pairs={{16,12},{17,13},{18,14},{19,15}} | collective-permute-start | bytes 491528 | tf_op jit(solution)/shard_map/ppermute | solution.py:237
  365.9 6.5 %collective-permute-start.70 = (bf16[32,2560]{1,0:T(8,128)(2,1)S(1)}, bf16[32,2560]{1,0:T(8,128)(2,1)S(1)}, u32[]{:S(2)}, u32[]{:S(2)}) collective-permute-start(bf16[32,2560]{1,0:T(8,128)(2,1)S(1)} %finish_bwd.9), channel_id=1, source_target_pairs={{16,12},{17,13},{18,14},{19,15}} | collective-permute-start | bytes 491528 | tf_op jit(solution)/shard_map/ppermute | solution.py:237
  386.4 19.0 %collective-permute-start.34 = (bf16[32,2560]{1,0:T(8,128)(2,1)S(1)}, bf16[32,2560]{1,0:T(8,128)(2,1)S(1)}, u32[]{:S(2)}, u32[]{:S(2)}) collective-permute-start(bf16[32,2560]{1,0:T(8,128)(2,1)S(1)} %finish_bwd.6), channel_id=1, source_target_pairs={{16,8},{17,9},{18,10},{19,11}} | collective-permute-start | bytes 491528 | tf_op jit(solution)/shard_map/ppermute | solution.py:237
  405.5 6.4 %collective-permute-start.75 = (bf16[32,2560]{1,0:T(8,128)(2,1)S(1)}, bf16[32,2560]{1,0:T(8,128)(2,1)S(1)}, u32[]{:S(2)}, u32[]{:S(2)}) collective-permute-start(bf16[32,2560]{1,0:T(8,128)(2,1)S(1)} %finish_bwd.9), channel_id=1, source_target_pairs={{16,8},{17,9},{18,10},{19,11}} | collective-permute-start | bytes 491528 | tf_op jit(solution)/shard_map/ppermute | solution.py:237
  431.2 22.9 %collective-permute-done.37.refs_0_ = bf16[64,2560]{1,0:T(8,128)(2,1)S(1)} collective-permute-done((bf16[64,2560]{1,0:T(8,128)(2,1)S(1)}, bf16[64,2560]{1,0:T(8,128)(2,1)S(1)}, u32[]{:S(2)}, u32[]{:S(2)}) %collective-permute-start.37) | collective-permute-done | bytes 327712 | tf_op jit(solution)/shard_map/ppermute | solution.py:237
  (237 shorter events, 199.1 us)
Async XLA Ops:
  2.4 21.2 %collective-permute-start = (bf16[1,16,2560]{2,1,0:T(8,128)(2,1)S(1)}, bf16[1,16,2560]{2,1,0:T(8,128)(2,1)S(1)}, u32[]{:S(2)}, u32[]{:S(2)}) collective-permute-start(bf16[1,16,2560]{2,1,0:T(8,128)(2,1)S(1)} %select_n.232), channel_id=1, source_target_pairs={{0,2},{1,3},{2,0},{3,1},{4,6},{5,7},{6,4},{7,5},{24,26},{25,27},{2... | collective-permute-start | bytes 245768 | tf_op jit(solution)/shard_map/ppermute | solution.py:237
  10.9 15.1 %collective-permute-start.41 = (bf16[1,16,2560]{2,1,0:T(8,128)(2,1)S(1)}, bf16[1,16,2560]{2,1,0:T(8,128)(2,1)S(1)}, u32[]{:S(2)}, u32[]{:S(2)}) collective-permute-start(bf16[1,16,2560]{2,1,0:T(8,128)(2,1)S(1)} %select_n.256), channel_id=1, source_target_pairs={{0,2},{1,3},{2,0},{3,1},{4,6},{5,7},{6,4},{7,5},{24,26},{25,27},{2... | collective-permute-start | bytes 245768 | tf_op jit(solution)/shard_map/ppermute | solution.py:237
  71.4 45.4 %collective-permute-start.10 = (bf16[32,2560]{1,0:T(8,128)(2,1)S(1)}, bf16[32,2560]{1,0:T(8,128)(2,1)S(1)}, u32[]{:S(2)}, u32[]{:S(2)}) collective-permute-start(bf16[32,2560]{1,0:T(8,128)(2,1)S(1)} %finish_fwd.6), channel_id=1, source_target_pairs={{4,12},{5,13},{6,14},{7,15}} | collective-permute-start | bytes 491528 | tf_op jit(solution)/shard_map/ppermute | solution.py:237
  72.1 51.2 %collective-permute-start.51 = (bf16[32,2560]{1,0:T(8,128)(2,1)S(1)}, bf16[32,2560]{1,0:T(8,128)(2,1)S(1)}, u32[]{:S(2)}, u32[]{:S(2)}) collective-permute-start(bf16[32,2560]{1,0:T(8,128)(2,1)S(1)} %finish_fwd.9), channel_id=1, source_target_pairs={{4,12},{5,13},{6,14},{7,15}} | collective-permute-start | bytes 491528 | tf_op jit(solution)/shard_map/ppermute | solution.py:237
  77.3 33.0 %collective-permute-start.49 = (bf16[32,2560]{1,0:T(8,128)(2,1)S(1)}, bf16[32,2560]{1,0:T(8,128)(2,1)S(1)}, u32[]{:S(2)}, u32[]{:S(2)}) collective-permute-start(bf16[32,2560]{1,0:T(8,128)(2,1)S(1)} %get-tuple-element.76), channel_id=1, source_target_pairs={{12,13},{13,12},{14,15},{15,14}} | collective-permute-start | bytes 491528 | tf_op jit(solution)/shard_map/ppermute | solution.py:237
  78.1 38.8 %collective-permute-start.9 = (bf16[32,2560]{1,0:T(8,128)(2,1)S(1)}, bf16[32,2560]{1,0:T(8,128)(2,1)S(1)}, u32[]{:S(2)}, u32[]{:S(2)}) collective-permute-start(bf16[32,2560]{1,0:T(8,128)(2,1)S(1)} %add_convert_fusion.12.refs_0_), channel_id=1, source_target_pairs={{12,14},{13,15},{14,12},{15,13}} | collective-permute-start | bytes 491528 | tf_op jit(solution)/shard_map/ppermute | solution.py:237
  130.5 15.8 %collective-permute-start.53 = (bf16[32,2560]{1,0:T(8,128)(2,1)S(1)}, bf16[32,2560]{1,0:T(8,128)(2,1)S(1)}, u32[]{:S(2)}, u32[]{:S(2)}) collective-permute-start(bf16[32,2560]{1,0:T(8,128)(2,1)S(1)} %collective-permute-done.52.refs_0_.refs_3_), channel_id=1, source_target_pairs={{16,17},{17,16},{18,19},{19,18}} | collective-permute-start | bytes 491528 | tf_op jit(solution)/shard_map/ppermute | solution.py:237
  134.6 22.2 %collective-permute-start.13 = (bf16[64,2560]{1,0:T(8,128)(2,1)S(1)}, bf16[64,2560]{1,0:T(8,128)(2,1)S(1)}, u32[]{:S(2)}, u32[]{:S(2)}) collective-permute-start(bf16[64,2560]{1,0:T(8,128)(2,1)S(1)} %get-tuple-element.55), channel_id=1, source_target_pairs={{16,20},{17,21},{18,22},{19,23}} | collective-permute-start | bytes 983048 | tf_op jit(solution)/shard_map/ppermute | solution.py:237
  150.4 24.8 %collective-permute-start.54 = (bf16[64,2560]{1,0:T(8,128)(2,1)S(1)}, bf16[64,2560]{1,0:T(8,128)(2,1)S(1)}, u32[]{:S(2)}, u32[]{:S(2)}) collective-permute-start(bf16[64,2560]{1,0:T(8,128)(2,1)S(1)} %get-tuple-element.77), channel_id=1, source_target_pairs={{16,20},{17,21},{18,22},{19,23}} | collective-permute-start | bytes 983048 | tf_op jit(solution)/shard_map/ppermute | solution.py:237
  161.3 19.1 %collective-permute-start.14 = (bf16[32,2560]{1,0:T(8,128)(2,1)S(1)}, bf16[32,2560]{1,0:T(8,128)(2,1)S(1)}, u32[]{:S(2)}, u32[]{:S(2)}) collective-permute-start(bf16[32,2560]{1,0:T(8,128)(2,1)S(1)} %get-tuple-element.57), channel_id=1, source_target_pairs={{20,21},{21,20},{22,23},{23,22}} | collective-permute-start | bytes 491528 | tf_op jit(solution)/shard_map/ppermute | solution.py:237
  162.0 31.6 %collective-permute-start.16 = (bf16[32,2560]{1,0:T(8,128)(2,1)S(1)}, bf16[32,2560]{1,0:T(8,128)(2,1)S(1)}, u32[]{:S(2)}, u32[]{:S(2)}) collective-permute-start(bf16[32,2560]{1,0:T(8,128)(2,1)S(1)} %finish_fwd.7), channel_id=1, source_target_pairs={{12,20},{13,21},{14,22},{15,23}} | collective-permute-start | bytes 491528 | tf_op jit(solution)/shard_map/ppermute | solution.py:237
  168.7 37.8 %collective-permute-start.57 = (bf16[32,2560]{1,0:T(8,128)(2,1)S(1)}, bf16[32,2560]{1,0:T(8,128)(2,1)S(1)}, u32[]{:S(2)}, u32[]{:S(2)}) collective-permute-start(bf16[32,2560]{1,0:T(8,128)(2,1)S(1)} %finish_fwd.10), channel_id=1, source_target_pairs={{12,20},{13,21},{14,22},{15,23}} | collective-permute-start | bytes 491528 | tf_op jit(solution)/shard_map/ppermute | solution.py:237
  187.2 19.3 %collective-permute-start.56 = (bf16[32,2560]{1,0:T(8,128)(2,1)S(1)}, bf16[32,2560]{1,0:T(8,128)(2,1)S(1)}, u32[]{:S(2)}, u32[]{:S(2)}) collective-permute-start(bf16[32,2560]{1,0:T(8,128)(2,1)S(1)} %add_convert_fusion.4.refs_0_), channel_id=1, source_target_pairs={{20,22},{21,23},{22,20},{23,21}} | collective-permute-start | bytes 491528 | tf_op jit(solution)/shard_map/ppermute | solution.py:237
  193.7 25.6 %collective-permute-start.17 = (bf16[32,2560]{1,0:T(8,128)(2,1)S(1)}, bf16[32,2560]{1,0:T(8,128)(2,1)S(1)}, u32[]{:S(2)}, u32[]{:S(2)}) collective-permute-start(bf16[32,2560]{1,0:T(8,128)(2,1)S(1)} %finish_fwd.8), channel_id=1, source_target_pairs={{20,24},{21,25},{22,26},{23,27}} | collective-permute-start | bytes 491528 | tf_op jit(solution)/shard_map/ppermute | solution.py:237
  200.1 19.2 %collective-permute-start.22 = (bf16[32,2560]{1,0:T(8,128)(2,1)S(1)}, bf16[32,2560]{1,0:T(8,128)(2,1)S(1)}, u32[]{:S(2)}, u32[]{:S(2)}) collective-permute-start(bf16[32,2560]{1,0:T(8,128)(2,1)S(1)} %finish_fwd.8), channel_id=1, source_target_pairs={{20,28},{21,29},{22,30},{23,31}} | collective-permute-start | bytes 491528 | tf_op jit(solution)/shard_map/ppermute | solution.py:237
  220.1 21.6 %collective-permute-start.59 = (bf16[32,2560]{1,0:T(8,128)(2,1)S(1)}, bf16[32,2560]{1,0:T(8,128)(2,1)S(1)}, u32[]{:S(2)}, u32[]{:S(2)}) collective-permute-start(bf16[32,2560]{1,0:T(8,128)(2,1)S(1)} %get-tuple-element.98.refs_1_.refs_4_), channel_id=1, source_target_pairs={{24,25},{25,24},{26,27},{27,26},{28,29},{29,28},{30,31},{31,30}} | collective-permute-start | bytes 491528 | tf_op jit(solution)/shard_map/ppermute | solution.py:237
  229.0 23.2 %collective-permute-start.19 = (bf16[64,2560]{1,0:T(8,128)(2,1)S(1)}, bf16[64,2560]{1,0:T(8,128)(2,1)S(1)}, u32[]{:S(2)}, u32[]{:S(2)}) collective-permute-start(bf16[64,2560]{1,0:T(8,128)(2,1)S(1)} %get-tuple-element.58), channel_id=1, source_target_pairs={{24,28},{25,29},{26,30},{27,31},{28,24},{29,25},{30,26},{31,27}} | collective-permute-start | bytes 983048 | tf_op jit(solution)/shard_map/ppermute | solution.py:237
  263.0 18.6 %collective-permute-start.21 = (bf16[32,2560]{1,0:T(8,128)(2,1)S(1)}, bf16[32,2560]{1,0:T(8,128)(2,1)S(1)}, u32[]{:S(2)}, u32[]{:S(2)}) collective-permute-start(bf16[32,2560]{1,0:T(8,128)(2,1)S(1)} %add_convert_fusion.10.refs_1_), channel_id=1, source_target_pairs={{28,30},{29,31},{30,28},{31,29},{24,26},{25,27},{26,24},{27,25}} | collective-permute-start | bytes 491528 | tf_op jit(solution)/shard_map/ppermute | solution.py:237
  296.5 16.4 %collective-permute-start.65 = (bf16[32,2560]{1,0:T(8,128)(2,1)S(1)}, bf16[32,2560]{1,0:T(8,128)(2,1)S(1)}, u32[]{:S(2)}, u32[]{:S(2)}) collective-permute-start(bf16[32,2560]{1,0:T(8,128)(2,1)S(1)} %collective-permute-done.64.refs_0_), channel_id=1, source_target_pairs={{20,21},{21,20},{22,23},{23,22}} | collective-permute-start | bytes 491528 | tf_op jit(solution)/shard_map/ppermute | solution.py:237
  300.1 22.1 %collective-permute-start.25 = (bf16[64,2560]{1,0:T(8,128)(2,1)S(1)}, bf16[64,2560]{1,0:T(8,128)(2,1)S(1)}, u32[]{:S(2)}, u32[]{:S(2)}) collective-permute-start(bf16[64,2560]{1,0:T(8,128)(2,1)S(1)} %first_bwd.6), channel_id=1, source_target_pairs={{20,16},{21,17},{22,18},{23,19}} | collective-permute-start | bytes 983048 | tf_op jit(solution)/shard_map/ppermute | solution.py:237
  315.8 24.8 %collective-permute-start.66 = (bf16[64,2560]{1,0:T(8,128)(2,1)S(1)}, bf16[64,2560]{1,0:T(8,128)(2,1)S(1)}, u32[]{:S(2)}, u32[]{:S(2)}) collective-permute-start(bf16[64,2560]{1,0:T(8,128)(2,1)S(1)} %first_bwd.9), channel_id=1, source_target_pairs={{20,16},{21,17},{22,18},{23,19}} | collective-permute-start | bytes 983048 | tf_op jit(solution)/shard_map/ppermute | solution.py:237
  326.9 19.0 %collective-permute-start.26 = (bf16[32,2560]{1,0:T(8,128)(2,1)S(1)}, bf16[32,2560]{1,0:T(8,128)(2,1)S(1)}, u32[]{:S(2)}, u32[]{:S(2)}) collective-permute-start(bf16[32,2560]{1,0:T(8,128)(2,1)S(1)} %get-tuple-element.64), channel_id=1, source_target_pairs={{16,17},{17,16},{18,19},{19,18}} | collective-permute-start | bytes 491528 | tf_op jit(solution)/shard_map/ppermute | solution.py:237
  327.6 31.2 %collective-permute-start.28 = (bf16[32,2560]{1,0:T(8,128)(2,1)S(1)}, bf16[32,2560]{1,0:T(8,128)(2,1)S(1)}, u32[]{:S(2)}, u32[]{:S(2)}) collective-permute-start(bf16[32,2560]{1,0:T(8,128)(2,1)S(1)} %finish_mix.2), channel_id=1, source_target_pairs={{24,16},{25,17},{26,18},{27,19}} | collective-permute-start | bytes 491528 | tf_op jit(solution)/shard_map/ppermute | solution.py:237
  334.2 31.3 %collective-permute-start.69 = (bf16[32,2560]{1,0:T(8,128)(2,1)S(1)}, bf16[32,2560]{1,0:T(8,128)(2,1)S(1)}, u32[]{:S(2)}, u32[]{:S(2)}) collective-permute-start(bf16[32,2560]{1,0:T(8,128)(2,1)S(1)} %finish_mix.3), channel_id=1, source_target_pairs={{24,16},{25,17},{26,18},{27,19}} | collective-permute-start | bytes 491528 | tf_op jit(solution)/shard_map/ppermute | solution.py:237
  380.4 31.5 %collective-permute-start.72 = (bf16[64,2560]{1,0:T(8,128)(2,1)S(1)}, bf16[64,2560]{1,0:T(8,128)(2,1)S(1)}, u32[]{:S(2)}, u32[]{:S(2)}) collective-permute-start(bf16[64,2560]{1,0:T(8,128)(2,1)S(1)} %first_bwd.10), channel_id=1, source_target_pairs={{12,8},{13,9},{14,10},{15,11}} | collective-permute-start | bytes 983048 | tf_op jit(solution)/shard_map/ppermute | solution.py:237
  385.8 31.5 %collective-permute-start.32 = (bf16[32,2560]{1,0:T(8,128)(2,1)S(1)}, bf16[32,2560]{1,0:T(8,128)(2,1)S(1)}, u32[]{:S(2)}, u32[]{:S(2)}) collective-permute-start(bf16[32,2560]{1,0:T(8,128)(2,1)S(1)} %get-tuple-element.67), channel_id=1, source_target_pairs={{8,9},{9,8},{10,11},{11,10}} | collective-permute-start | bytes 491528 | tf_op jit(solution)/shard_map/ppermute | solution.py:237
  386.4 32.2 %collective-permute-start.34 = (bf16[32,2560]{1,0:T(8,128)(2,1)S(1)}, bf16[32,2560]{1,0:T(8,128)(2,1)S(1)}, u32[]{:S(2)}, u32[]{:S(2)}) collective-permute-start(bf16[32,2560]{1,0:T(8,128)(2,1)S(1)} %finish_bwd.6), channel_id=1, source_target_pairs={{16,8},{17,9},{18,10},{19,11}} | collective-permute-start | bytes 491528 | tf_op jit(solution)/shard_map/ppermute | solution.py:237
  425.0 29.1 %collective-permute-start.37 = (bf16[64,2560]{1,0:T(8,128)(2,1)S(1)}, bf16[64,2560]{1,0:T(8,128)(2,1)S(1)}, u32[]{:S(2)}, u32[]{:S(2)}) collective-permute-start(bf16[64,2560]{1,0:T(8,128)(2,1)S(1)} %first_bwd.8), channel_id=1, source_target_pairs={{4,0},{5,1},{6,2},{7,3}} | collective-permute-start | bytes 983048 | tf_op jit(solution)/shard_map/ppermute | solution.py:237
  429.9 33.4 %collective-permute-start.78 = (bf16[64,2560]{1,0:T(8,128)(2,1)}, bf16[64,2560]{1,0:T(8,128)(2,1)}, u32[]{:S(2)}, u32[]{:S(2)}) collective-permute-start(bf16[64,2560]{1,0:T(8,128)(2,1)} %first_bwd.11), channel_id=1, source_target_pairs={{4,0},{5,1},{6,2},{7,3}} | collective-permute-start | bytes 983048 | tf_op jit(solution)/shard_map/ppermute | solution.py:237
  458.7 17.3 %collective-permute-start.38 = (bf16[32,2560]{1,0:T(8,128)(2,1)S(1)}, bf16[32,2560]{1,0:T(8,128)(2,1)S(1)}, u32[]{:S(2)}, u32[]{:S(2)}) collective-permute-start(bf16[32,2560]{1,0:T(8,128)(2,1)S(1)} %get-tuple-element.70), channel_id=1, source_target_pairs={{0,1},{1,0},{2,3},{3,2}} | collective-permute-start | bytes 491528 | tf_op jit(solution)/shard_map/ppermute | solution.py:237
  460.7 21.3 %collective-permute-start.40 = (bf16[32,2560]{1,0:T(8,128)(2,1)S(1)}, bf16[32,2560]{1,0:T(8,128)(2,1)S(1)}, u32[]{:S(2)}, u32[]{:S(2)}) collective-permute-start(bf16[32,2560]{1,0:T(8,128)(2,1)S(1)} %finish_bwd.7), channel_id=1, source_target_pairs={{8,0},{9,1},{10,2},{11,3}} | collective-permute-start | bytes 491528 | tf_op jit(solution)/shard_map/ppermute | solution.py:237
  462.0 22.9 %collective-permute-start.81 = (bf16[32,2560]{1,0:T(8,128)(2,1)S(1)}, bf16[32,2560]{1,0:T(8,128)(2,1)S(1)}, u32[]{:S(2)}, u32[]{:S(2)}) collective-permute-start(bf16[32,2560]{1,0:T(8,128)(2,1)S(1)} %finish_bwd.10), channel_id=1, source_target_pairs={{8,0},{9,1},{10,2},{11,3}} | collective-permute-start | bytes 491528 | tf_op jit(solution)/shard_map/ppermute | solution.py:237
  (67 other events, 840.2 us)
where the time goes:
time: 490 us; the launch traced here: 489 us
  starting transfers between devices  319 us (65%)
  Pallas kernels  114 us (23%)
  waiting for transfers between devices  33.1 us (7%)
  local copies, waits for them, and re-layouts  16 us (3%)
    ppermute x82, starting transfers between devices, send(): return lax.ppermute(x, AXES, route)  319 us
    pallas_call x14, Pallas kernels, second(): pl.pallas_call(functools.partial(second_kernel, mode, tile_of(D)), in_spe...  65.6 us
    pallas_call x14, Pallas kernels, first(): pl.pallas_call(functools.partial(first_kernel, mode, tile_of(F)), in_spec...  45.2 us
    ppermute x82, waiting for transfers between devices, send(): return lax.ppermute(x, AXES, route)  33.1 us
    unnamed x34, local copies, waits for them, and re-layouts  15.7 us
  transfers between devices with their start and end apart: 82, of which 5 were waited for; matrix products, arithmetic and copies ran while one was open for 0% of the time, Pallas kernels for 23%

commit v1 on v0

v1 whole, which is shorter than its diff:
```python
import functools

import jax
import jax.numpy as jnp
from jax import lax
from jax.experimental import pallas as pl
from jax.experimental.pallas import tpu as pltpu
from jax.sharding import PartitionSpec as P

LAYERS = 4
epsilon = 1e-05
AXES = ("section", "tensor")
f32, bf16 = jnp.float32, jnp.bfloat16
VMEM = pl.BlockSpec(memory_space=pltpu.VMEM)
SMEM = pl.BlockSpec(memory_space=pltpu.SMEM)
HBM = pl.BlockSpec(memory_space=pltpu.HBM)


def params(mib=4):
    return pltpu.CompilerParams(vmem_limit_bytes=mib * 1024 * 1024)


def tile_of(width):
    for tile in (512, 256, 128):
        if width % tile == 0:
            return tile
    return width


def gelu_both(v):
    c = 0.7978845608028654
    v2 = v * v
    th = jnp.tanh(c * v * (1.0 + 0.044715 * v2))
    half = 0.5 * (1.0 + th)
    slope = half + 0.5 * v * (1.0 - th * th) * (c * (1.0 + 3 * 0.044715 * v2))
    return v * half, slope


def inverse_rms_of(rows):
    return lax.rsqrt(jnp.mean(rows * rows, axis=-1, keepdims=True) + epsilon)


def load_weights(w, roles):
    def kernel(src, given, dst, kept, sem):
        copy = pltpu.make_async_copy(src, dst, sem)
        copy.start()
        for i in range(roles.shape[0]):
            kept[i] = given[i]
        copy.wait()

    return pl.pallas_call(
        kernel,
        in_specs=[HBM, SMEM],
        out_specs=[VMEM, SMEM],
        out_shape=[pltpu.VMEM(w.shape, w.dtype), pltpu.SMEM(roles.shape, roles.dtype)],
        scratch_shapes=[pltpu.SemaphoreType.DMA(())],
        compiler_params=params(2),
        name="load_weights",
    )(w, roles)


def first_kernel(mode, at, tile, flag, *refs):
    @pl.when(flag[at] != 0)
    def _():
        first_active(mode, at, tile, flag, *refs)


def first_active(mode, at, tile, flag, *refs):
    up = None
    if mode == "bwd":
        part, got, w, out, a = refs
    else:
        part, got, gain, w, out, slope, a = refs
        if mode == "mix":
            up = flag[at] == 1
    h = part.shape[0]
    for i, ref in enumerate((part, got)):
        if mode == "bwd":
            a[i * h:(i + 1) * h] = ref[...]
        else:
            x = ref[...].astype(f32)
            n = (x * inverse_rms_of(x) * gain[...]).astype(bf16)
            if up is not None:
                n = jnp.where(up, n, ref[...])
            a[i * h:(i + 1) * h] = n

    def step(i, carry):
        cols = pl.ds(pl.multiple_of(i * tile, tile), tile)
        y = jnp.dot(a[...], w[:, cols], preferred_element_type=f32)
        if mode == "bwd":
            out[:, cols] = y.astype(bf16)
        else:
            value, grad = gelu_both(y)
            slope[:, cols] = grad.astype(bf16)
            if up is not None:
                value = jnp.where(up, value, y)
            out[:, cols] = value.astype(bf16)
        return carry

    lax.fori_loop(0, w.shape[1] // tile, step, 0)


def first(mode, at, flag, part, got, gain, w):
    rows = 2 * part.shape[0]
    D, F = w.shape
    shape = jax.ShapeDtypeStruct((rows, F), bf16)
    args = (flag, part, got, w) if mode == "bwd" else (flag, part, got, gain, w)
    count = 1 if mode == "bwd" else 2
    return pl.pallas_call(
        functools.partial(first_kernel, mode, at, tile_of(F)),
        in_specs=[SMEM] + [VMEM] * (len(args) - 1),
        out_specs=[VMEM] * count,
        out_shape=[shape] * count,
        scratch_shapes=[pltpu.VMEM((rows, D), bf16)],
        compiler_params=params(),
        cost_estimate=pl.CostEstimate(
            flops=2 * rows * D * F, bytes_accessed=2 * D * F, transcendentals=rows * F
        ),
        name="first_" + mode,
    )(*args)


def second_kernel(mode, at, tile, flag, *refs):
    @pl.when(flag[at] != 0)
    def _():
        second_active(mode, at, tile, flag, *refs)


def second_active(mode, at, tile, flag, *refs):
    if mode == "fwd":
        arrived, w, keep, give, a = refs
    else:
        arrived, slope, w, keep, give, a = refs
    if mode == "fwd":
        a = arrived
    else:
        z = arrived[...]
        d = (z.astype(f32) * slope[...].astype(f32)).astype(bf16)
        if mode == "mix":
            d = jnp.where(flag[at] == 1, d, z)
        a[...] = d
    h = keep.shape[0]

    def step(i, carry):
        cols = pl.ds(pl.multiple_of(i * tile, tile), tile)
        y = lax.dot_general(
            a[...], w[cols, :], (((1,), (1,)), ((), ())), preferred_element_type=f32
        )
        keep[:, cols] = y[:h]
        give[:, cols] = y[h:].astype(bf16)
        return carry

    lax.fori_loop(0, w.shape[0] // tile, step, 0)


def second(mode, at, flag, arrived, slope, w):
    rows, F = arrived.shape
    D = w.shape[0]
    args = (flag, arrived, w) if mode == "fwd" else (flag, arrived, slope, w)
    return pl.pallas_call(
        functools.partial(second_kernel, mode, at, tile_of(D)),
        in_specs=[SMEM] + [VMEM] * (len(args) - 1),
        out_specs=[VMEM] * 2,
        out_shape=[
            jax.ShapeDtypeStruct((rows // 2, D), f32),
            jax.ShapeDtypeStruct((rows // 2, D), bf16),
        ],
        scratch_shapes=[pltpu.VMEM((rows, F), bf16)],
        compiler_params=params(),
        cost_estimate=pl.CostEstimate(
            flops=2 * rows * D * F, bytes_accessed=2 * D * F, transcendentals=0
        ),
        name="second_" + mode,
    )(*args)


def finish_kernel(mode, at, *refs):
    if mode == "fwd":
        total, got, rest, out = refs
        out[...] = (
            rest[...].astype(f32) + (total[...].astype(f32) + got[...].astype(f32))
        ).astype(bf16)
        return
    if mode == "bwd":
        total, got, rest, saved, gain, out = refs
    else:
        flag, total, got, rest, saved, gain, out = refs
    summed = total[...].astype(f32) + got[...].astype(f32)
    x = saved[...].astype(f32)
    scale = inverse_rms_of(x)
    unit = x * scale
    gu = summed * gain[...]
    delta = scale * (gu - unit * jnp.mean(gu * unit, axis=-1, keepdims=True))
    if mode == "mix":
        delta = jnp.where(flag[at] == 1, delta, summed)
    out[...] = (rest[...].astype(f32) + delta).astype(bf16)


def finish(mode, at, flag, total, got, rest, saved, gain):
    args = {
        "fwd": (total, got, rest),
        "bwd": (total, got, rest, saved, gain),
    }.get(mode, (flag, total, got, rest, saved, gain))
    specs = [VMEM] * len(args)
    if mode == "mix":
        specs[0] = SMEM
    return pl.pallas_call(
        functools.partial(finish_kernel, mode, at),
        in_specs=specs,
        out_specs=VMEM,
        out_shape=jax.ShapeDtypeStruct(rest.shape, bf16),
        compiler_params=params(),
        name="finish_" + mode,
    )(*args)


def body(inputs, cotangent, weights, norm_gains):
    S = lax.axis_size("section")
    T = lax.axis_size("tensor")
    stacks = S // (2 * LAYERS)
    stride = 2 * stacks
    si = lax.axis_index("section")
    ti = lax.axis_index("tensor")
    group = si % stride // 2
    layer = si // stride
    up = si % 2 == 0
    D = weights.shape[1]
    B = inputs.shape[0] // stacks
    share = inputs.shape[1] // D
    hi = T // 2
    h = hi * share
    top = 2 * (LAYERS - 1)
    bits = T.bit_length() - 1

    def send(x, pairs, flip=0):
        route = [(a * T + t, b * T + (t ^ flip)) for a, b in pairs for t in range(T)]
        return lax.ppermute(x, AXES, route)

    def section(k, q, down):
        return k * stride + 2 * q + down

    def each(pairs):
        return [(section(a, q, i), section(b, q, j)) for a, i, b, j in pairs for q in range(stacks)]

    steps = top + 1
    gain = lax.dynamic_index_in_dim(norm_gains, group * LAYERS + layer, 0, keepdims=True)
    own_in = lax.dynamic_slice_in_dim(inputs, group * B, B, 0)
    own_cot = lax.dynamic_slice_in_dim(cotangent, group * B, B, 0)
    own = jnp.where(layer == 0, own_in, own_cot).reshape(B, share, D)
    tick = jnp.arange(steps, dtype=jnp.int32)
    ahead = tick == layer
    behind = tick == top - layer
    roles = jnp.concatenate([
        jnp.where(up, jnp.where(ahead, 1, 0), jnp.where(behind, 2, 0)),
        jnp.where(up, jnp.where(behind, 1, 0), jnp.where(ahead, 2, 0)),
    ]).astype(jnp.int32)
    oks = [jnp.where(up, top - layer, layer) == t for t in range(steps)]
    last = layer == LAYERS - 1
    seed_main, seed_rest = last & ~up, last & up
    high = ti // 2
    highs = [(ti >> bit) % 2 == 1 for bit in range(1, bits)]
    w, own, gain, roles, oks, seed_main, seed_rest, high, highs = lax.optimization_barrier(
        (weights[0], own, gain, roles, oks, seed_main, seed_rest, high, highs)
    )

    def spread(x, users):
        x = x[None]
        for bit in range(1, bits):
            got = send(x, users, 1 << bit)
            got, _ = lax.optimization_barrier((got, roles))
            x = jnp.where(
                highs[bit - 1], jnp.concatenate([got, x], 0), jnp.concatenate([x, got], 0)
            )
        return x.reshape(h, D)

    everyone = [(s, s) for s in range(S)]
    w, roles = load_weights(w, roles)
    seed = []
    for b in range(B):
        seed.append(spread(own[b], everyone))
    main = list(seed)
    rest = list(seed)
    saved = [[None] * LAYERS for _ in range(B)]
    slopes = [[None] * LAYERS for _ in range(B)]
    results = [jnp.zeros((share, D), bf16) for _ in range(B)]

    for t in range(top + 1):
        forward = t < LAYERS
        backward = t >= LAYERS - 1
        mode = "mix" if forward and backward else ("fwd" if forward else "bwd")
        k, j = t, top - t
        swap, cross, along = [], [], []
        if forward:
            swap.append((k, 0, k, 1))
            if k + 1 < LAYERS:
                cross.append((k, 1, k + 1, 0))
                along.append((k, 1, k + 1, 1))
        if backward:
            swap.append((j, 1, j, 0))
            if j > 0:
                cross.append((j, 0, j - 1, 1))
                along.append((j, 0, j - 1, 0))
        swap, cross, along = each(swap), each(cross), each(along)
        if t == LAYERS - 1:
            main = [jnp.where(seed_main, seed[b], main[b]) for b in range(B)]
            rest = [jnp.where(seed_rest, seed[b], rest[b]) for b in range(B)]
        arrived = []
        for b in range(B):
            got = send(main[b], everyone, 1)
            if forward:
                saved[b][k] = main[b]
                out, slopes[b][k] = first(mode, t, roles, main[b], got, gain, w)
            else:
                (out,) = first(mode, t, roles, main[b], got, gain, w)
            arrived.append(send(out, swap))
        fresh = []
        for b in range(B):
            _, _, arrived[b] = lax.optimization_barrier((rest[b], fresh[-1:], arrived[b]))
            keep, give = second(
                mode, steps + t, roles, arrived[b], slopes[b][j] if backward else None, w
            )
            total = keep + send(give, everyone, 1).astype(f32)
            for bit in range(1, bits):
                mine = total.astype(bf16)
                got = send(mine, everyone, 1 << bit)
                if bit < bits - 1:
                    total = mine.astype(f32) + got.astype(f32)
            fresh.append(
                finish(mode, steps + t, roles, mine, got, rest[b], saved[b][j] if backward else None, gain)
            )
        for b in range(B):
            mine = lax.dynamic_index_in_dim(
                fresh[b].reshape(hi, share, D), high, 0, keepdims=False
            )
            results[b] = jnp.where(oks[t], mine, results[b])
        if t < top:
            main = [send(fresh[b], cross) for b in range(B)]
            rest = [send(fresh[b], along) for b in range(B)]
    return jnp.stack(results).reshape(1, B, share * D)


def solution(mesh):
    placed = (P(None, "tensor"), P(None, "tensor"), P("section", None, "tensor"), P())
    return jax.shard_map(
        body, mesh=mesh, in_specs=placed, out_specs=P("section", None, "tensor"), check_vma=False
    )
```

time: 490 us -> 307 us (0.63)
  starting transfers between devices: 319 us -> 51.7 us
  waiting for transfers between devices: 33.1 us -> 226 us
  Pallas kernels: 114 us -> 20.3 us
  local copies, waits for them, and re-layouts: 16 us -> 4.86 us
    ppermute x82, starting transfers between devices: 319 us -> 51.7 us  [send(): return lax.ppermute(x, AXES, route)]
    ppermute x82, waiting for transfers between devices: 33.1 us -> 226 us  [send(): return lax.ppermute(x, AXES, route)]
    pallas_call x43, Pallas kernels: 114 us -> 20.3 us  [the longest x14 9.36 us: second(): pl.pallas_call(functools.partial(second_kernel, mode, at, tile_of(D)), in...]
    unnamed x34 -> x5, local copies, waits for them, and re-layouts: 15.7 us -> 4.75 us
  transfers between devices with their start and end apart: 82 -> 82, of which waited for: 5 -> 32; matrix products, arithmetic and copies ran while one was open for 0% -> 0% of each run, Pallas kernels for 23% -> 4%
where the time goes in v1:
time: 307 us; the launch traced here: 306 us
  waiting for transfers between devices  226 us (74%)
  starting transfers between devices  51.7 us (17%)
  Pallas kernels  20.3 us (7%)
  local copies, waits for them, and re-layouts  4.86 us (2%)
    ppermute x82, waiting for transfers between devices, send(): return lax.ppermute(x, AXES, route)  226 us
    ppermute x82, starting transfers between devices, send(): return lax.ppermute(x, AXES, route)  51.7 us
    pallas_call x14, Pallas kernels, second(): pl.pallas_call(functools.partial(second_kernel, mode, at, tile_of(D)), in...  9.36 us
    pallas_call x14, Pallas kernels, first(): pl.pallas_call(functools.partial(first_kernel, mode, at, tile_of(F)), in_...  6.78 us
  transfers between devices with their start and end apart: 82, of which 32 were waited for; matrix products, arithmetic and copies ran while one was open for 0% of the time, Pallas kernels for 4%

profile of v1, /device:TPU:0, one launch (start us, length us, event | category | flops | bytes accessed | tf_op | source)
XLA Modules:
  0.0 306.4 jit_solution(7883666525271301173)
XLA Ops:
  1.3 3.1 %collective-permute-start = (bf16[1,16,2560]{2,1,0:T(8,128)(2,1)S(1)}, bf16[1,16,2560]{2,1,0:T(8,128)(2,1)S(1)}, u32[]{:S(2)}, u32[]{:S(2)}) collective-permute-start(bf16[1,16,2560]{2,1,0:T(8,128)(2,1)S(1)} %get-tuple-element.163), channel_id=1, source_target_pairs={{0,2},{1,3},{2,0},{3,1},{4,6},{5,7},{6,4},{7,5},{8,10},{9,11},{10,... | collective-permute-start | bytes 245768 | tf_op jit(solution)/shard_map/ppermute | solution.py:237
  4.3 4.7 %copy-done.1 = bf16[1,2560,2560]{2,1,0:T(8,128)(2,1)S(1)} copy-done((bf16[1,2560,2560]{2,1,0:T(8,128)(2,1)S(1)}, bf16[1,2560,2560]{2,1,0:T(8,128)(2,1)}, u32[]{:S(2)}) %copy-start.1) | copy-done | bytes 13107224
  9.1 1.4 load_weights.1
  10.7 4.8 %collective-permute-done.41 = bf16[1,16,2560]{2,1,0:T(8,128)(2,1)S(1)} collective-permute-done((bf16[1,16,2560]{2,1,0:T(8,128)(2,1)S(1)}, bf16[1,16,2560]{2,1,0:T(8,128)(2,1)S(1)}, u32[]{:S(2)}, u32[]{:S(2)}) %collective-permute-start.41) | collective-permute-done | bytes 81952 | tf_op jit(solution)/shard_map/ppermute | solution.py:237
  15.5 3.4 %first_fwd.6 = (bf16[64,2560]{1,0:T(8,128)(2,1)S(1)}, bf16[64,2560]{1,0:T(8,128)(2,1)S(1)}) custom-call(s32[14]{0:T(128)S(4)} %get-tuple-element.85.flag.refs_0_, bf16[32,2560]{1,0:T(8,128)(2,1)S(1)} %bitcast.31, bf16[32,2560]{1,0:T(8,128)(2,1)S(1)} %collective-permute-done.1.refs_1_, f32[1,2560]{1,0:T(1,128)S(1)} %constant_dynamic-slice_fusion.refs_2_.refs_5_.refs_4_, ...), custom_call_target="tpu_custom_call" | custom-call | flops 838860800 | bytes 13107200 | tf_op jit(solution)/shard_map/first_fwd/pallas_call | solution.py:109
  18.9 1.3 collective-permute-start.2
  20.3 6.8 %collective-permute-done.2.refs_0_ = bf16[64,2560]{1,0:T(8,128)(2,1)S(1)} collective-permute-done((bf16[64,2560]{1,0:T(8,128)(2,1)S(1)}, bf16[64,2560]{1,0:T(8,128)(2,1)S(1)}, u32[]{:S(2)}, u32[]{:S(2)}) %collective-permute-start.2) | collective-permute-done | bytes 327712 | tf_op jit(solution)/shard_map/ppermute | solution.py:237
  27.1 3.4 %first_fwd.9 = (bf16[64,2560]{1,0:T(8,128)(2,1)S(1)}, bf16[64,2560]{1,0:T(8,128)(2,1)S(1)}) custom-call(s32[14]{0:T(128)S(4)} %get-tuple-element.85.flag.refs_0_, bf16[32,2560]{1,0:T(8,128)(2,1)S(1)} %bitcast.27, bf16[32,2560]{1,0:T(8,128)(2,1)S(1)} %collective-permute-done.42.refs_1_, f32[1,2560]{1,0:T(1,128)S(1)} %constant_dynamic-slice_fusion.refs_2_.refs_5_.refs_4_, ...), custom_call_target="tpu_custom_call" | custom-call | flops 838860800 | bytes 13107200 | tf_op jit(solution)/shard_map/first_fwd/pallas_call | solution.py:109
  30.5 5.7 %collective-permute-start.43 = (bf16[64,2560]{1,0:T(8,128)(2,1)S(1)}, bf16[64,2560]{1,0:T(8,128)(2,1)S(1)}, u32[]{:S(2)}, u32[]{:S(2)}) collective-permute-start(bf16[64,2560]{1,0:T(8,128)(2,1)S(1)} %get-tuple-element.130), channel_id=1, source_target_pairs={{0,4},{1,5},{2,6},{3,7}} | collective-permute-start | bytes 983048 | tf_op jit(solution)/shard_map/ppermute | solution.py:237
  36.9 5.7 %collective-permute-done.4.refs_1_ = bf16[32,2560]{1,0:T(8,128)(2,1)S(1)} collective-permute-done((bf16[32,2560]{1,0:T(8,128)(2,1)S(1)}, bf16[32,2560]{1,0:T(8,128)(2,1)S(1)}, u32[]{:S(2)}, u32[]{:S(2)}) %collective-permute-start.4) | collective-permute-done | bytes 163872 | tf_op jit(solution)/shard_map/ppermute | solution.py:237
  46.5 5.0 %collective-permute-done.45.refs_1_ = bf16[32,2560]{1,0:T(8,128)(2,1)S(1)} collective-permute-done((bf16[32,2560]{1,0:T(8,128)(2,1)S(1)}, bf16[32,2560]{1,0:T(8,128)(2,1)S(1)}, u32[]{:S(2)}, u32[]{:S(2)}) %collective-permute-start.45) | collective-permute-done | bytes 163872 | tf_op jit(solution)/shard_map/ppermute | solution.py:237
  56.4 5.0 %collective-permute-done.10.refs_1_ = bf16[32,2560]{1,0:T(8,128)(2,1)S(1)} collective-permute-done((bf16[32,2560]{1,0:T(8,128)(2,1)S(1)}, bf16[32,2560]{1,0:T(8,128)(2,1)S(1)}, u32[]{:S(2)}, u32[]{:S(2)}) %collective-permute-start.10) | collective-permute-done | bytes 163872 | tf_op jit(solution)/shard_map/ppermute | solution.py:237
  65.0 5.0 %collective-permute-done.51.refs_1_ = bf16[32,2560]{1,0:T(8,128)(2,1)S(1)} collective-permute-done((bf16[32,2560]{1,0:T(8,128)(2,1)S(1)}, bf16[32,2560]{1,0:T(8,128)(2,1)S(1)}, u32[]{:S(2)}, u32[]{:S(2)}) %collective-permute-start.51) | collective-permute-done | bytes 163872 | tf_op jit(solution)/shard_map/ppermute | solution.py:237
  74.9 5.0 %collective-permute-done.16.refs_1_ = bf16[32,2560]{1,0:T(8,128)(2,1)S(1)} collective-permute-done((bf16[32,2560]{1,0:T(8,128)(2,1)S(1)}, bf16[32,2560]{1,0:T(8,128)(2,1)S(1)}, u32[]{:S(2)}, u32[]{:S(2)}) %collective-permute-start.16) | collective-permute-done | bytes 163872 | tf_op jit(solution)/shard_map/ppermute | solution.py:237
  82.5 5.7 %collective-permute-done.57.refs_1_ = bf16[32,2560]{1,0:T(8,128)(2,1)S(1)} collective-permute-done((bf16[32,2560]{1,0:T(8,128)(2,1)S(1)}, bf16[32,2560]{1,0:T(8,128)(2,1)S(1)}, u32[]{:S(2)}, u32[]{:S(2)}) %collective-permute-start.57) | collective-permute-done | bytes 163872 | tf_op jit(solution)/shard_map/ppermute | solution.py:237
  93.4 5.7 %collective-permute-done.22.refs_2_ = bf16[32,2560]{1,0:T(8,128)(2,1)S(1)} collective-permute-done((bf16[32,2560]{1,0:T(8,128)(2,1)S(1)}, bf16[32,2560]{1,0:T(8,128)(2,1)S(1)}, u32[]{:S(2)}, u32[]{:S(2)}) %collective-permute-start.22) | collective-permute-done | bytes 163872 | tf_op jit(solution)/shard_map/ppermute | solution.py:237
  103.0 5.0 %collective-permute-done.63.refs_2_ = bf16[32,2560]{1,0:T(8,128)(2,1)S(1)} collective-permute-done((bf16[32,2560]{1,0:T(8,128)(2,1)S(1)}, bf16[32,2560]{1,0:T(8,128)(2,1)S(1)}, u32[]{:S(2)}, u32[]{:S(2)}) %collective-permute-start.63) | collective-permute-done | bytes 163872 | tf_op jit(solution)/shard_map/ppermute | solution.py:237
  113.1 5.0 %collective-permute-done.28.refs_1_ = bf16[32,2560]{1,0:T(8,128)(2,1)S(1)} collective-permute-done((bf16[32,2560]{1,0:T(8,128)(2,1)S(1)}, bf16[32,2560]{1,0:T(8,128)(2,1)S(1)}, u32[]{:S(2)}, u32[]{:S(2)}) %collective-permute-start.28) | collective-permute-done | bytes 163872 | tf_op jit(solution)/shard_map/ppermute | solution.py:237
  122.0 5.0 %collective-permute-done.69.refs_1_ = bf16[32,2560]{1,0:T(8,128)(2,1)S(1)} collective-permute-done((bf16[32,2560]{1,0:T(8,128)(2,1)S(1)}, bf16[32,2560]{1,0:T(8,128)(2,1)S(1)}, u32[]{:S(2)}, u32[]{:S(2)}) %collective-permute-start.69) | collective-permute-done | bytes 163872 | tf_op jit(solution)/shard_map/ppermute | solution.py:237
  132.1 5.0 %collective-permute-done.34.refs_1_ = bf16[32,2560]{1,0:T(8,128)(2,1)S(1)} collective-permute-done((bf16[32,2560]{1,0:T(8,128)(2,1)S(1)}, bf16[32,2560]{1,0:T(8,128)(2,1)S(1)}, u32[]{:S(2)}, u32[]{:S(2)}) %collective-permute-start.34) | collective-permute-done | bytes 163872 | tf_op jit(solution)/shard_map/ppermute | solution.py:237
  140.3 1.3 collective-permute-start.38
  141.6 4.4 %collective-permute-done.75.refs_1_ = bf16[32,2560]{1,0:T(8,128)(2,1)S(1)} collective-permute-done((bf16[32,2560]{1,0:T(8,128)(2,1)S(1)}, bf16[32,2560]{1,0:T(8,128)(2,1)S(1)}, u32[]{:S(2)}, u32[]{:S(2)}) %collective-permute-start.75) | collective-permute-done | bytes 163872 | tf_op jit(solution)/shard_map/ppermute | solution.py:237
  146.9 1.3 collective-permute-start.35
  148.3 127.5 %collective-permute-done.35.refs_2_ = bf16[32,2560]{1,0:T(8,128)(2,1)S(1)} collective-permute-done((bf16[32,2560]{1,0:T(8,128)(2,1)S(1)}, bf16[32,2560]{1,0:T(8,128)(2,1)S(1)}, u32[]{:S(2)}, u32[]{:S(2)}) %collective-permute-start.35) | collective-permute-done | bytes 163872 | tf_op jit(solution)/shard_map/ppermute | solution.py:237
  275.8 4.6 %second_bwd.8 = (f32[32,2560]{1,0:T(8,128)S(1)}, bf16[32,2560]{1,0:T(8,128)(2,1)S(1)}) custom-call(s32[14]{0:T(128)S(4)} %get-tuple-element.85.flag.refs_0_, bf16[64,2560]{1,0:T(8,128)(2,1)S(1)} %collective-permute-done.38.refs_0_, bf16[64,2560]{1,0:T(8,128)(2,1)S(1)} %get-tuple-element.119.refs_1_, ...), custom_call_target="tpu_custom_call" | custom-call | flops 838860800 | bytes 13107200 | tf_op jit(solution)/shard_map/second_bwd/pallas_call | solution.py:160
  280.6 1.3 collective-permute-start.79
  283.9 4.7 %collective-permute-done.40.refs_1_ = bf16[32,2560]{1,0:T(8,128)(2,1)S(1)} collective-permute-done((bf16[32,2560]{1,0:T(8,128)(2,1)S(1)}, bf16[32,2560]{1,0:T(8,128)(2,1)S(1)}, u32[]{:S(2)}, u32[]{:S(2)}) %collective-permute-start.40) | collective-permute-done | bytes 163872 | tf_op jit(solution)/shard_map/ppermute | solution.py:237
  288.9 1.9 collective-permute-done.76.refs_2_
  290.7 1.8 collective-permute-done.79.refs_0_
  292.5 4.6 %second_bwd.11 = (f32[32,2560]{1,0:T(8,128)S(1)}, bf16[32,2560]{1,0:T(8,128)(2,1)S(1)}) custom-call(s32[14]{0:T(128)S(4)} %get-tuple-element.85.flag.refs_0_, bf16[64,2560]{1,0:T(8,128)(2,1)S(1)} %collective-permute-done.79.refs_0_, bf16[64,2560]{1,0:T(8,128)(2,1)S(1)} %get-tuple-element.156.refs_1_, ...), custom_call_target="tpu_custom_call" | custom-call | flops 838860800 | bytes 13107200 | tf_op jit(solution)/shard_map/second_bwd/pallas_call | solution.py:160
  297.2 1.4 collective-permute-done.80
  299.4 5.6 %collective-permute-done.81.refs_1_ = bf16[32,2560]{1,0:T(8,128)(2,1)S(1)} collective-permute-done((bf16[32,2560]{1,0:T(8,128)(2,1)S(1)}, bf16[32,2560]{1,0:T(8,128)(2,1)S(1)}, u32[]{:S(2)}, u32[]{:S(2)}) %collective-permute-start.81) | collective-permute-done | bytes 163872 | tf_op jit(solution)/shard_map/ppermute | solution.py:237
  (208 shorter events, 53.1 us)
Async XLA Ops:
  1.3 9.2 %collective-permute-start = (bf16[1,16,2560]{2,1,0:T(8,128)(2,1)S(1)}, bf16[1,16,2560]{2,1,0:T(8,128)(2,1)S(1)}, u32[]{:S(2)}, u32[]{:S(2)}) collective-permute-start(bf16[1,16,2560]{2,1,0:T(8,128)(2,1)S(1)} %get-tuple-element.163), channel_id=1, source_target_pairs={{0,2},{1,3},{2,0},{3,1},{4,6},{5,7},{6,4},{7,5},{8,10},{9,11},{10,... | collective-permute-start | bytes 245768 | tf_op jit(solution)/shard_map/ppermute | solution.py:237
  18.9 8.3 %collective-permute-start.2 = (bf16[64,2560]{1,0:T(8,128)(2,1)S(1)}, bf16[64,2560]{1,0:T(8,128)(2,1)S(1)}, u32[]{:S(2)}, u32[]{:S(2)}) collective-permute-start(bf16[64,2560]{1,0:T(8,128)(2,1)S(1)} %get-tuple-element.92), channel_id=1, source_target_pairs={{0,4},{1,5},{2,6},{3,7}} | collective-permute-start | bytes 983048 | tf_op jit(solution)/shard_map/ppermute | solution.py:237
  20.2 6.9 %collective-permute-start.42 = (bf16[32,2560]{1,0:T(8,128)(2,1)S(1)}, bf16[32,2560]{1,0:T(8,128)(2,1)S(1)}, u32[]{:S(2)}, u32[]{:S(2)}) collective-permute-start(bf16[32,2560]{1,0:T(8,128)(2,1)S(1)} %bitcast.26), channel_id=1, source_target_pairs={{0,1},{1,0},{2,3},{3,2},{4,5},{5,4},{6,7},{7,6},{8,9},{9,8},{10,11... | collective-permute-start | bytes 491528 | tf_op jit(solution)/shard_map/ppermute | solution.py:237
  27.1 9.1 %collective-permute-start.3 = (bf16[32,2560]{1,0:T(8,128)(2,1)S(1)}, bf16[32,2560]{1,0:T(8,128)(2,1)S(1)}, u32[]{:S(2)}, u32[]{:S(2)}) collective-permute-start(bf16[32,2560]{1,0:T(8,128)(2,1)S(1)} %get-tuple-element.95), channel_id=1, source_target_pairs={{0,1},{1,0},{2,3},{3,2},{4,5},{5,4},{6,7},{7,6},{8,9},{9,8},{10,11... | collective-permute-start | bytes 491528 | tf_op jit(solution)/shard_map/ppermute | solution.py:237
  30.5 13.2 %collective-permute-start.43 = (bf16[64,2560]{1,0:T(8,128)(2,1)S(1)}, bf16[64,2560]{1,0:T(8,128)(2,1)S(1)}, u32[]{:S(2)}, u32[]{:S(2)}) collective-permute-start(bf16[64,2560]{1,0:T(8,128)(2,1)S(1)} %get-tuple-element.130), channel_id=1, source_target_pairs={{0,4},{1,5},{2,6},{3,7}} | collective-permute-start | bytes 983048 | tf_op jit(solution)/shard_map/ppermute | solution.py:237
  36.2 6.3 %collective-permute-start.4 = (bf16[32,2560]{1,0:T(8,128)(2,1)S(1)}, bf16[32,2560]{1,0:T(8,128)(2,1)S(1)}, u32[]{:S(2)}, u32[]{:S(2)}) collective-permute-start(bf16[32,2560]{1,0:T(8,128)(2,1)S(1)} %add_convert_fusion.13.refs_0_), channel_id=1, source_target_pairs={{0,2},{1,3},{2,0},{3,1},{4,6},{5,7},{6,4},{7,5},{8,10},{9,11},{10,... | collective-permute-start | bytes 491528 | tf_op jit(solution)/shard_map/ppermute | solution.py:237
  45.2 6.3 %collective-permute-start.45 = (bf16[32,2560]{1,0:T(8,128)(2,1)S(1)}, bf16[32,2560]{1,0:T(8,128)(2,1)S(1)}, u32[]{:S(2)}, u32[]{:S(2)}) collective-permute-start(bf16[32,2560]{1,0:T(8,128)(2,1)S(1)} %add_convert_fusion.6.refs_0_), channel_id=1, source_target_pairs={{0,2},{1,3},{2,0},{3,1},{4,6},{5,7},{6,4},{7,5},{8,10},{9,11},{10,... | collective-permute-start | bytes 491528 | tf_op jit(solution)/shard_map/ppermute | solution.py:237
  45.8 7.2 %collective-permute-start.8 = (bf16[64,2560]{1,0:T(8,128)(2,1)S(1)}, bf16[64,2560]{1,0:T(8,128)(2,1)S(1)}, u32[]{:S(2)}, u32[]{:S(2)}) collective-permute-start(bf16[64,2560]{1,0:T(8,128)(2,1)S(1)} %get-tuple-element.96), channel_id=1, source_target_pairs={{8,12},{9,13},{10,14},{11,15}} | collective-permute-start | bytes 983048 | tf_op jit(solution)/shard_map/ppermute | solution.py:237
  54.4 7.8 %collective-permute-start.49 = (bf16[64,2560]{1,0:T(8,128)(2,1)S(1)}, bf16[64,2560]{1,0:T(8,128)(2,1)S(1)}, u32[]{:S(2)}, u32[]{:S(2)}) collective-permute-start(bf16[64,2560]{1,0:T(8,128)(2,1)S(1)} %get-tuple-element.134), channel_id=1, source_target_pairs={{8,12},{9,13},{10,14},{11,15}} | collective-permute-start | bytes 983048 | tf_op jit(solution)/shard_map/ppermute | solution.py:237
  55.1 6.3 %collective-permute-start.10 = (bf16[32,2560]{1,0:T(8,128)(2,1)S(1)}, bf16[32,2560]{1,0:T(8,128)(2,1)S(1)}, u32[]{:S(2)}, u32[]{:S(2)}) collective-permute-start(bf16[32,2560]{1,0:T(8,128)(2,1)S(1)} %add_convert_fusion.12.refs_0_), channel_id=1, source_target_pairs={{0,2},{1,3},{2,0},{3,1},{4,6},{5,7},{6,4},{7,5},{8,10},{9,11},{10,... | collective-permute-start | bytes 491528 | tf_op jit(solution)/shard_map/ppermute | solution.py:237
  55.7 6.4 %collective-permute-start.46 = (bf16[32,2560]{1,0:T(8,128)(2,1)S(1)}, bf16[32,2560]{1,0:T(8,128)(2,1)S(1)}, u32[]{:S(2)}, u32[]{:S(2)}) collective-permute-start(bf16[32,2560]{1,0:T(8,128)(2,1)S(1)} %finish_fwd.9), channel_id=1, source_target_pairs={{4,12},{5,13},{6,14},{7,15}} | collective-permute-start | bytes 491528 | tf_op jit(solution)/shard_map/ppermute | solution.py:237
  63.7 6.3 %collective-permute-start.51 = (bf16[32,2560]{1,0:T(8,128)(2,1)S(1)}, bf16[32,2560]{1,0:T(8,128)(2,1)S(1)}, u32[]{:S(2)}, u32[]{:S(2)}) collective-permute-start(bf16[32,2560]{1,0:T(8,128)(2,1)S(1)} %add_convert_fusion.5.refs_0_), channel_id=1, source_target_pairs={{0,2},{1,3},{2,0},{3,1},{4,6},{5,7},{6,4},{7,5},{8,10},{9,11},{10,... | collective-permute-start | bytes 491528 | tf_op jit(solution)/shard_map/ppermute | solution.py:237
  64.3 7.2 %collective-permute-start.14 = (bf16[64,2560]{1,0:T(8,128)(2,1)S(1)}, bf16[64,2560]{1,0:T(8,128)(2,1)S(1)}, u32[]{:S(2)}, u32[]{:S(2)}) collective-permute-start(bf16[64,2560]{1,0:T(8,128)(2,1)S(1)} %get-tuple-element.100), channel_id=1, source_target_pairs={{16,20},{17,21},{18,22},{19,23}} | collective-permute-start | bytes 983048 | tf_op jit(solution)/shard_map/ppermute | solution.py:237
  72.9 7.1 %collective-permute-start.55 = (bf16[64,2560]{1,0:T(8,128)(2,1)S(1)}, bf16[64,2560]{1,0:T(8,128)(2,1)S(1)}, u32[]{:S(2)}, u32[]{:S(2)}) collective-permute-start(bf16[64,2560]{1,0:T(8,128)(2,1)S(1)} %get-tuple-element.138), channel_id=1, source_target_pairs={{16,20},{17,21},{18,22},{19,23}} | collective-permute-start | bytes 983048 | tf_op jit(solution)/shard_map/ppermute | solution.py:237
  73.7 6.3 %collective-permute-start.16 = (bf16[32,2560]{1,0:T(8,128)(2,1)S(1)}, bf16[32,2560]{1,0:T(8,128)(2,1)S(1)}, u32[]{:S(2)}, u32[]{:S(2)}) collective-permute-start(bf16[32,2560]{1,0:T(8,128)(2,1)S(1)} %add_convert_fusion.11.refs_0_), channel_id=1, source_target_pairs={{0,2},{1,3},{2,0},{3,1},{4,6},{5,7},{6,4},{7,5},{8,10},{9,11},{10,... | collective-permute-start | bytes 491528 | tf_op jit(solution)/shard_map/ppermute | solution.py:237
  81.6 6.6 %collective-permute-start.57 = (bf16[32,2560]{1,0:T(8,128)(2,1)S(1)}, bf16[32,2560]{1,0:T(8,128)(2,1)S(1)}, u32[]{:S(2)}, u32[]{:S(2)}) collective-permute-start(bf16[32,2560]{1,0:T(8,128)(2,1)S(1)} %add_convert_fusion.4.refs_0_), channel_id=1, source_target_pairs={{0,2},{1,3},{2,0},{3,1},{4,6},{5,7},{6,4},{7,5},{8,10},{9,11},{10,... | collective-permute-start | bytes 491528 | tf_op jit(solution)/shard_map/ppermute | solution.py:237
  82.3 7.4 %collective-permute-start.19 = (bf16[32,2560]{1,0:T(8,128)(2,1)S(1)}, bf16[32,2560]{1,0:T(8,128)(2,1)S(1)}, u32[]{:S(2)}, u32[]{:S(2)}) collective-permute-start(bf16[32,2560]{1,0:T(8,128)(2,1)S(1)} %get-tuple-element.161.refs_0_.refs_4_), channel_id=1, source_target_pairs={{0,1},{1,0},{2,3},{3,2},{4,5},{5,4},{6,7},{7,6},{8,9},{9,8},{10,11... | collective-permute-start | bytes 491528 | tf_op jit(solution)/shard_map/ppermute | solution.py:237
  91.9 8.2 %collective-permute-start.61 = (bf16[64,2560]{1,0:T(8,128)(2,1)S(1)}, bf16[64,2560]{1,0:T(8,128)(2,1)S(1)}, u32[]{:S(2)}, u32[]{:S(2)}) collective-permute-start(bf16[64,2560]{1,0:T(8,128)(2,1)S(1)} %get-tuple-element.142), channel_id=1, source_target_pairs={{24,28},{25,29},{26,30},{27,31},{28,24},{29,25},{30,26},{31,27}} | collective-permute-start | bytes 983048 | tf_op jit(solution)/shard_map/ppermute | solution.py:237
  92.8 6.3 %collective-permute-start.22 = (bf16[32,2560]{1,0:T(8,128)(2,1)S(1)}, bf16[32,2560]{1,0:T(8,128)(2,1)S(1)}, u32[]{:S(2)}, u32[]{:S(2)}) collective-permute-start(bf16[32,2560]{1,0:T(8,128)(2,1)S(1)} %add_convert_fusion.10.refs_1_), channel_id=1, source_target_pairs={{0,2},{1,3},{2,0},{3,1},{4,6},{5,7},{6,4},{7,5},{8,10},{9,11},{10,... | collective-permute-start | bytes 491528 | tf_op jit(solution)/shard_map/ppermute | solution.py:237
  102.3 7.5 %collective-permute-start.26 = (bf16[64,2560]{1,0:T(8,128)(2,1)S(1)}, bf16[64,2560]{1,0:T(8,128)(2,1)S(1)}, u32[]{:S(2)}, u32[]{:S(2)}) collective-permute-start(bf16[64,2560]{1,0:T(8,128)(2,1)S(1)} %first_bwd.6), channel_id=1, source_target_pairs={{20,16},{21,17},{22,18},{23,19}} | collective-permute-start | bytes 983048 | tf_op jit(solution)/shard_map/ppermute | solution.py:237
  111.1 8.0 %collective-permute-start.67 = (bf16[64,2560]{1,0:T(8,128)(2,1)S(1)}, bf16[64,2560]{1,0:T(8,128)(2,1)S(1)}, u32[]{:S(2)}, u32[]{:S(2)}) collective-permute-start(bf16[64,2560]{1,0:T(8,128)(2,1)S(1)} %first_bwd.9), channel_id=1, source_target_pairs={{20,16},{21,17},{22,18},{23,19}} | collective-permute-start | bytes 983048 | tf_op jit(solution)/shard_map/ppermute | solution.py:237
  111.8 6.3 %collective-permute-start.28 = (bf16[32,2560]{1,0:T(8,128)(2,1)S(1)}, bf16[32,2560]{1,0:T(8,128)(2,1)S(1)}, u32[]{:S(2)}, u32[]{:S(2)}) collective-permute-start(bf16[32,2560]{1,0:T(8,128)(2,1)S(1)} %add_convert_fusion.9.refs_0_), channel_id=1, source_target_pairs={{0,2},{1,3},{2,0},{3,1},{4,6},{5,7},{6,4},{7,5},{8,10},{9,11},{10,... | collective-permute-start | bytes 491528 | tf_op jit(solution)/shard_map/ppermute | solution.py:237
  112.5 6.7 %collective-permute-start.64 = (bf16[32,2560]{1,0:T(8,128)(2,1)S(1)}, bf16[32,2560]{1,0:T(8,128)(2,1)S(1)}, u32[]{:S(2)}, u32[]{:S(2)}) collective-permute-start(bf16[32,2560]{1,0:T(8,128)(2,1)S(1)} %finish_mix.3), channel_id=1, source_target_pairs={{24,16},{25,17},{26,18},{27,19}} | collective-permute-start | bytes 491528 | tf_op jit(solution)/shard_map/ppermute | solution.py:237
  121.3 7.4 %collective-permute-start.32 = (bf16[64,2560]{1,0:T(8,128)(2,1)S(1)}, bf16[64,2560]{1,0:T(8,128)(2,1)S(1)}, u32[]{:S(2)}, u32[]{:S(2)}) collective-permute-start(bf16[64,2560]{1,0:T(8,128)(2,1)S(1)} %first_bwd.7), channel_id=1, source_target_pairs={{12,8},{13,9},{14,10},{15,11}} | collective-permute-start | bytes 983048 | tf_op jit(solution)/shard_map/ppermute | solution.py:237
  130.1 8.0 %collective-permute-start.73 = (bf16[64,2560]{1,0:T(8,128)(2,1)S(1)}, bf16[64,2560]{1,0:T(8,128)(2,1)S(1)}, u32[]{:S(2)}, u32[]{:S(2)}) collective-permute-start(bf16[64,2560]{1,0:T(8,128)(2,1)S(1)} %first_bwd.10), channel_id=1, source_target_pairs={{12,8},{13,9},{14,10},{15,11}} | collective-permute-start | bytes 983048 | tf_op jit(solution)/shard_map/ppermute | solution.py:237
  131.4 6.7 %collective-permute-start.70 = (bf16[32,2560]{1,0:T(8,128)(2,1)S(1)}, bf16[32,2560]{1,0:T(8,128)(2,1)S(1)}, u32[]{:S(2)}, u32[]{:S(2)}) collective-permute-start(bf16[32,2560]{1,0:T(8,128)(2,1)S(1)} %finish_bwd.9), channel_id=1, source_target_pairs={{16,8},{17,9},{18,10},{19,11}} | collective-permute-start | bytes 491528 | tf_op jit(solution)/shard_map/ppermute | solution.py:237
  140.3 135.6 %collective-permute-start.38 = (bf16[64,2560]{1,0:T(8,128)(2,1)S(1)}, bf16[64,2560]{1,0:T(8,128)(2,1)S(1)}, u32[]{:S(2)}, u32[]{:S(2)}) collective-permute-start(bf16[64,2560]{1,0:T(8,128)(2,1)S(1)} %first_bwd.8), channel_id=1, source_target_pairs={{4,0},{5,1},{6,2},{7,3}} | collective-permute-start | bytes 983048 | tf_op jit(solution)/shard_map/ppermute | solution.py:237
  146.9 128.9 %collective-permute-start.35 = (bf16[32,2560]{1,0:T(8,128)(2,1)S(1)}, bf16[32,2560]{1,0:T(8,128)(2,1)S(1)}, u32[]{:S(2)}, u32[]{:S(2)}) collective-permute-start(bf16[32,2560]{1,0:T(8,128)(2,1)S(1)} %finish_bwd.7), channel_id=1, source_target_pairs={{8,0},{9,1},{10,2},{11,3}} | collective-permute-start | bytes 491528 | tf_op jit(solution)/shard_map/ppermute | solution.py:237
  148.2 132.3 %collective-permute-start.78 = (bf16[32,2560]{1,0:T(8,128)(2,1)S(1)}, bf16[32,2560]{1,0:T(8,128)(2,1)S(1)}, u32[]{:S(2)}, u32[]{:S(2)}) collective-permute-start(bf16[32,2560]{1,0:T(8,128)(2,1)S(1)} %collective-permute-done.77.refs_0_), channel_id=1, source_target_pairs={{0,1},{1,0},{2,3},{3,2},{4,5},{5,4},{6,7},{7,6},{8,9},{9,8},{10,11... | collective-permute-start | bytes 491528 | tf_op jit(solution)/shard_map/ppermute | solution.py:237
  280.6 12.0 %collective-permute-start.79 = (bf16[64,2560]{1,0:T(8,128)(2,1)S(1)}, bf16[64,2560]{1,0:T(8,128)(2,1)S(1)}, u32[]{:S(2)}, u32[]{:S(2)}) collective-permute-start(bf16[64,2560]{1,0:T(8,128)(2,1)S(1)} %first_bwd.11), channel_id=1, source_target_pairs={{4,0},{5,1},{6,2},{7,3}} | collective-permute-start | bytes 983048 | tf_op jit(solution)/shard_map/ppermute | solution.py:237
  282.0 6.6 %collective-permute-start.40 = (bf16[32,2560]{1,0:T(8,128)(2,1)S(1)}, bf16[32,2560]{1,0:T(8,128)(2,1)S(1)}, u32[]{:S(2)}, u32[]{:S(2)}) collective-permute-start(bf16[32,2560]{1,0:T(8,128)(2,1)S(1)} %add_convert_fusion.7.refs_0_), channel_id=1, source_target_pairs={{0,2},{1,3},{2,0},{3,1},{4,6},{5,7},{6,4},{7,5},{8,10},{9,11},{10,... | collective-permute-start | bytes 491528 | tf_op jit(solution)/shard_map/ppermute | solution.py:237
  282.6 8.1 %collective-permute-start.76 = (bf16[32,2560]{1,0:T(8,128)(2,1)S(1)}, bf16[32,2560]{1,0:T(8,128)(2,1)S(1)}, u32[]{:S(2)}, u32[]{:S(2)}) collective-permute-start(bf16[32,2560]{1,0:T(8,128)(2,1)S(1)} %finish_bwd.10), channel_id=1, source_target_pairs={{8,0},{9,1},{10,2},{11,3}} | collective-permute-start | bytes 491528 | tf_op jit(solution)/shard_map/ppermute | solution.py:237
  (52 other events, 114.9 us)

commit v2 on v1

--- a/solution.py
+++ b/solution.py
@@ -6,6 +6,7 @@
 from jax.experimental import pallas as pl
 from jax.experimental.pallas import tpu as pltpu
 from jax.sharding import PartitionSpec as P
+
 
 LAYERS = 4
 epsilon = 1e-05
@@ -116,7 +117,6 @@
         cost_estimate=pl.CostEstimate(
             flops=2 * rows * D * F, bytes_accessed=2 * D * F, transcendentals=rows * F
         ),
-        name="first_" + mode,
     )(*args)
 
 
@@ -170,7 +170,6 @@
         cost_estimate=pl.CostEstimate(
             flops=2 * rows * D * F, bytes_accessed=2 * D * F, transcendentals=0
         ),
-        name="second_" + mode,
     )(*args)
 
 
@@ -210,7 +209,6 @@
         out_specs=VMEM,
         out_shape=jax.ShapeDtypeStruct(rest.shape, bf16),
         compiler_params=params(),
-        name="finish_" + mode,
     )(*args)
 
 
@@ -263,11 +261,11 @@
         (weights[0], own, gain, roles, oks, seed_main, seed_rest, high, highs)
     )
 
-    def spread(x, users):
+    def spread(x, users, gate):
         x = x[None]
         for bit in range(1, bits):
             got = send(x, users, 1 << bit)
-            got, _ = lax.optimization_barrier((got, roles))
+            got, _ = lax.optimization_barrier((got, gate))
             x = jnp.where(
                 highs[bit - 1], jnp.concatenate([got, x], 0), jnp.concatenate([x, got], 0)
             )
@@ -275,16 +273,14 @@
 
     everyone = [(s, s) for s in range(S)]
     w, roles = load_weights(w, roles)
-    seed = []
-    for b in range(B):
-        seed.append(spread(own[b], everyone))
+    seed = [spread(own[0], everyone, roles)] + [None] * (B - 1)
     main = list(seed)
     rest = list(seed)
     saved = [[None] * LAYERS for _ in range(B)]
     slopes = [[None] * LAYERS for _ in range(B)]
     results = [jnp.zeros((share, D), bf16) for _ in range(B)]
 
-    for t in range(top + 1):
+    def plan(t):
         forward = t < LAYERS
         backward = t >= LAYERS - 1
         mode = "mix" if forward and backward else ("fwd" if forward else "bwd")
@@ -300,42 +296,61 @@
             if j > 0:
                 cross.append((j, 0, j - 1, 1))
                 along.append((j, 0, j - 1, 0))
-        swap, cross, along = each(swap), each(cross), each(along)
+        return forward, backward, mode, k, j, each(swap), each(cross), each(along)
+
+    def phase_one(t, b):
+        forward, _, mode, k, _, _, _, _ = plan(t)
+        if t == 0 and b > 0:
+            seed[b] = main[b] = rest[b] = spread(own[b], everyone, outs[0])
         if t == LAYERS - 1:
-            main = [jnp.where(seed_main, seed[b], main[b]) for b in range(B)]
-            rest = [jnp.where(seed_rest, seed[b], rest[b]) for b in range(B)]
-        arrived = []
+            main[b] = jnp.where(seed_main, seed[b], main[b])
+        got = send(main[b], everyone, 1)
+        if forward:
+            saved[b][k] = main[b]
+            outs[b], slopes[b][k] = first(mode, t, roles, main[b], got, gain, w)
+        else:
+            (outs[b],) = first(mode, t, roles, main[b], got, gain, w)
+        if t == LAYERS - 1:
+            late, _ = lax.optimization_barrier((rest[b], outs[b]))
+            rest[b] = jnp.where(seed_rest, seed[b], late)
+
+    outs = [None] * B
+    phase_one(0, 0)
+    for t in range(top + 1):
+        _, backward, mode, _, j, swap, cross, along = plan(t)
+        arrived = send(outs[0], swap, 0)
+        gate = outs[0]
         for b in range(B):
-            got = send(main[b], everyone, 1)
-            if forward:
-                saved[b][k] = main[b]
-                out, slopes[b][k] = first(mode, t, roles, main[b], got, gain, w)
-            else:
-                (out,) = first(mode, t, roles, main[b], got, gain, w)
-            arrived.append(send(out, swap))
-        fresh = []
-        for b in range(B):
-            _, _, arrived[b] = lax.optimization_barrier((rest[b], fresh[-1:], arrived[b]))
+            if b + 1 < B:
+                phase_one(t, b + 1)
+            arrived = lax.optimization_barrier((arrived, rest[b], gate))[0]
             keep, give = second(
-                mode, steps + t, roles, arrived[b], slopes[b][j] if backward else None, w
+                mode, steps + t, roles, arrived, slopes[b][j] if backward else None, w
             )
+            if b + 1 < B:
+                arrived = send(outs[b + 1], swap, 0)
             total = keep + send(give, everyone, 1).astype(f32)
             for bit in range(1, bits):
                 mine = total.astype(bf16)
                 got = send(mine, everyone, 1 << bit)
                 if bit < bits - 1:
                     total = mine.astype(f32) + got.astype(f32)
-            fresh.append(
-                finish(mode, steps + t, roles, mine, got, rest[b], saved[b][j] if backward else None, gain)
+            fresh = finish(
+                mode, steps + t, roles, mine, got, rest[b],
+                saved[b][j] if backward else None, gain,
             )
-        for b in range(B):
-            mine = lax.dynamic_index_in_dim(
-                fresh[b].reshape(hi, share, D), high, 0, keepdims=False
+            gate = fresh
+            piece = lax.dynamic_index_in_dim(
+                fresh.reshape(hi, share, D), high, 0, keepdims=False
             )
-            results[b] = jnp.where(oks[t], mine, results[b])
-        if t < top:
-            main = [send(fresh[b], cross) for b in range(B)]
-            rest = [send(fresh[b], along) for b in range(B)]
+            results[b] = jnp.where(oks[t], piece, results[b])
+            if t < top:
+                if b > 0:
+                    fresh = lax.optimization_barrier((fresh, outs[0]))[0]
+                main[b] = send(fresh, cross, 0)
+                rest[b] = send(fresh, along, 0)
+                if b == 0:
+                    phase_one(t + 1, 0)
     return jnp.stack(results).reshape(1, B, share * D)
 
 

time: 307 us -> 294 us (0.958)
  waiting for transfers between devices: 226 us -> 208 us
  starting transfers between devices: 51.7 us -> 55.6 us
    ppermute x82, waiting for transfers between devices: 226 us -> 208 us  [send(): return lax.ppermute(x, AXES, route)]
    ppermute x82, starting transfers between devices: 51.7 us -> 55.6 us  [send(): return lax.ppermute(x, AXES, route)]
  transfers between devices with their start and end apart: 82 -> 82, of which waited for: 32 -> 33; matrix products, arithmetic and copies ran while one was open for 0% -> 0% of each run, Pallas kernels for 4% -> 5%
where the time goes in v2:
time: 294 us; the launch traced here: 293 us
  waiting for transfers between devices  208 us (71%)
  starting transfers between devices  55.6 us (19%)
  Pallas kernels  20.3 us (7%)
  local copies, waits for them, and re-layouts  4.86 us (2%)
  other arithmetic  2.97 us (1%)
    ppermute x82, waiting for transfers between devices, send(): return lax.ppermute(x, AXES, route)  208 us
    ppermute x82, starting transfers between devices, send(): return lax.ppermute(x, AXES, route)  55.6 us
    pallas_call x14, Pallas kernels, second(): pl.pallas_call(functools.partial(second_kernel, mode, at, tile_of(D)), in...  9.36 us
    pallas_call x14, Pallas kernels, first(): pl.pallas_call(functools.partial(first_kernel, mode, at, tile_of(F)), in_...  6.78 us
  transfers between devices with their start and end apart: 82, of which 33 were waited for; matrix products, arithmetic and copies ran while one was open for 0% of the time, Pallas kernels for 5%

profile of v2, /device:TPU:0, one launch (start us, length us, event | category | flops | bytes accessed | tf_op | source)
XLA Modules:
  0.0 293.2 jit_solution(1962940696896978234)
XLA Ops:
  1.3 3.1 %collective-permute-start = (bf16[1,16,2560]{2,1,0:T(8,128)(2,1)S(1)}, bf16[1,16,2560]{2,1,0:T(8,128)(2,1)S(1)}, u32[]{:S(2)}, u32[]{:S(2)}) collective-permute-start(bf16[1,16,2560]{2,1,0:T(8,128)(2,1)S(1)} %get-tuple-element.175), channel_id=1, source_target_pairs={{0,2},{1,3},{2,0},{3,1},{4,6},{5,7},{6,4},{7,5},{8,10},{9,11},{10,... | collective-permute-start | bytes 245768 | tf_op jit(solution)/shard_map/ppermute | solution.py:235
  4.3 4.7 %copy-done.1 = bf16[1,2560,2560]{2,1,0:T(8,128)(2,1)S(1)} copy-done((bf16[1,2560,2560]{2,1,0:T(8,128)(2,1)S(1)}, bf16[1,2560,2560]{2,1,0:T(8,128)(2,1)}, u32[]{:S(2)}) %copy-start.1) | copy-done | bytes 13107224
  9.1 1.4 load_weights.1
  10.7 1.3 collective-permute-done.1.refs_1_
  12.0 3.4 %shard_map.46 = (bf16[64,2560]{1,0:T(8,128)(2,1)S(1)}, bf16[64,2560]{1,0:T(8,128)(2,1)S(1)}) custom-call(s32[14]{0:T(128)S(4)} %get-tuple-element.93.flag.refs_0_, bf16[32,2560]{1,0:T(8,128)(2,1)S(1)} %bitcast.31, bf16[32,2560]{1,0:T(8,128)(2,1)S(1)} %collective-permute-done.1.refs_1_, f32[1,2560]{1,0:T(1,128)S(1)} %constant_dynamic-slice_fusion.refs_2_.refs_5_.refs_4_, ...), custom_call_target="tpu_custom_call" | custom-call | flops 838860800 | bytes 13107200 | tf_op jit(solution)/shard_map/pallas_call | solution.py:110
  15.4 1.3 collective-permute-start.2
  16.9 7.3 %collective-permute-done.2.refs_0_ = bf16[64,2560]{1,0:T(8,128)(2,1)S(1)} collective-permute-done((bf16[64,2560]{1,0:T(8,128)(2,1)S(1)}, bf16[64,2560]{1,0:T(8,128)(2,1)S(1)}, u32[]{:S(2)}, u32[]{:S(2)}) %collective-permute-start.2) | collective-permute-done | bytes 327712 | tf_op jit(solution)/shard_map/ppermute | solution.py:235
  24.2 3.4 %shard_map.67 = (bf16[64,2560]{1,0:T(8,128)(2,1)S(1)}, bf16[64,2560]{1,0:T(8,128)(2,1)S(1)}) custom-call(s32[14]{0:T(128)S(4)} %get-tuple-element.93.flag.refs_0_, bf16[32,2560]{1,0:T(8,128)(2,1)S(1)} %bitcast.27, bf16[32,2560]{1,0:T(8,128)(2,1)S(1)} %collective-permute-done.42.refs_1_, f32[1,2560]{1,0:T(1,128)S(1)} %constant_dynamic-slice_fusion.refs_2_.refs_5_.refs_4_, ...), custom_call_target="tpu_custom_call" | custom-call | flops 838860800 | bytes 13107200 | tf_op jit(solution)/shard_map/pallas_call | solution.py:110
  27.6 5.7 %collective-permute-start.43 = (bf16[64,2560]{1,0:T(8,128)(2,1)S(1)}, bf16[64,2560]{1,0:T(8,128)(2,1)S(1)}, u32[]{:S(2)}, u32[]{:S(2)}) collective-permute-start(bf16[64,2560]{1,0:T(8,128)(2,1)S(1)} %get-tuple-element.139), channel_id=1, source_target_pairs={{0,4},{1,5},{2,6},{3,7}} | collective-permute-start | bytes 983048 | tf_op jit(solution)/shard_map/ppermute | solution.py:235
  34.1 5.6 %collective-permute-done.4.refs_1_ = bf16[32,2560]{1,0:T(8,128)(2,1)S(1)} collective-permute-done((bf16[32,2560]{1,0:T(8,128)(2,1)S(1)}, bf16[32,2560]{1,0:T(8,128)(2,1)S(1)}, u32[]{:S(2)}, u32[]{:S(2)}) %collective-permute-start.4) | collective-permute-done | bytes 163872 | tf_op jit(solution)/shard_map/ppermute | solution.py:235
  43.7 4.8 %collective-permute-done.45.refs_1_ = bf16[32,2560]{1,0:T(8,128)(2,1)S(1)} collective-permute-done((bf16[32,2560]{1,0:T(8,128)(2,1)S(1)}, bf16[32,2560]{1,0:T(8,128)(2,1)S(1)}, u32[]{:S(2)}, u32[]{:S(2)}) %collective-permute-start.45) | collective-permute-done | bytes 163872 | tf_op jit(solution)/shard_map/ppermute | solution.py:235
  53.7 4.9 %collective-permute-done.10.refs_1_ = bf16[32,2560]{1,0:T(8,128)(2,1)S(1)} collective-permute-done((bf16[32,2560]{1,0:T(8,128)(2,1)S(1)}, bf16[32,2560]{1,0:T(8,128)(2,1)S(1)}, u32[]{:S(2)}, u32[]{:S(2)}) %collective-permute-start.10) | collective-permute-done | bytes 163872 | tf_op jit(solution)/shard_map/ppermute | solution.py:235
  62.3 4.8 %collective-permute-done.51.refs_1_ = bf16[32,2560]{1,0:T(8,128)(2,1)S(1)} collective-permute-done((bf16[32,2560]{1,0:T(8,128)(2,1)S(1)}, bf16[32,2560]{1,0:T(8,128)(2,1)S(1)}, u32[]{:S(2)}, u32[]{:S(2)}) %collective-permute-start.51) | collective-permute-done | bytes 163872 | tf_op jit(solution)/shard_map/ppermute | solution.py:235
  72.2 4.9 %collective-permute-done.16.refs_1_ = bf16[32,2560]{1,0:T(8,128)(2,1)S(1)} collective-permute-done((bf16[32,2560]{1,0:T(8,128)(2,1)S(1)}, bf16[32,2560]{1,0:T(8,128)(2,1)S(1)}, u32[]{:S(2)}, u32[]{:S(2)}) %collective-permute-start.16) | collective-permute-done | bytes 163872 | tf_op jit(solution)/shard_map/ppermute | solution.py:235
  81.5 4.1 %collective-permute-done.57.refs_1_ = bf16[32,2560]{1,0:T(8,128)(2,1)S(1)} collective-permute-done((bf16[32,2560]{1,0:T(8,128)(2,1)S(1)}, bf16[32,2560]{1,0:T(8,128)(2,1)S(1)}, u32[]{:S(2)}, u32[]{:S(2)}) %collective-permute-start.57) | collective-permute-done | bytes 163872 | tf_op jit(solution)/shard_map/ppermute | solution.py:235
  90.4 5.5 %collective-permute-done.22.refs_2_ = bf16[32,2560]{1,0:T(8,128)(2,1)S(1)} collective-permute-done((bf16[32,2560]{1,0:T(8,128)(2,1)S(1)}, bf16[32,2560]{1,0:T(8,128)(2,1)S(1)}, u32[]{:S(2)}, u32[]{:S(2)}) %collective-permute-start.22) | collective-permute-done | bytes 163872 | tf_op jit(solution)/shard_map/ppermute | solution.py:235
  99.9 4.8 %collective-permute-done.63.refs_2_ = bf16[32,2560]{1,0:T(8,128)(2,1)S(1)} collective-permute-done((bf16[32,2560]{1,0:T(8,128)(2,1)S(1)}, bf16[32,2560]{1,0:T(8,128)(2,1)S(1)}, u32[]{:S(2)}, u32[]{:S(2)}) %collective-permute-start.63) | collective-permute-done | bytes 163872 | tf_op jit(solution)/shard_map/ppermute | solution.py:235
  110.1 4.9 %collective-permute-done.28.refs_1_ = bf16[32,2560]{1,0:T(8,128)(2,1)S(1)} collective-permute-done((bf16[32,2560]{1,0:T(8,128)(2,1)S(1)}, bf16[32,2560]{1,0:T(8,128)(2,1)S(1)}, u32[]{:S(2)}, u32[]{:S(2)}) %collective-permute-start.28) | collective-permute-done | bytes 163872 | tf_op jit(solution)/shard_map/ppermute | solution.py:235
  118.9 4.8 %collective-permute-done.69.refs_1_ = bf16[32,2560]{1,0:T(8,128)(2,1)S(1)} collective-permute-done((bf16[32,2560]{1,0:T(8,128)(2,1)S(1)}, bf16[32,2560]{1,0:T(8,128)(2,1)S(1)}, u32[]{:S(2)}, u32[]{:S(2)}) %collective-permute-start.69) | collective-permute-done | bytes 163872 | tf_op jit(solution)/shard_map/ppermute | solution.py:235
  129.0 4.9 %collective-permute-done.34.refs_1_ = bf16[32,2560]{1,0:T(8,128)(2,1)S(1)} collective-permute-done((bf16[32,2560]{1,0:T(8,128)(2,1)S(1)}, bf16[32,2560]{1,0:T(8,128)(2,1)S(1)}, u32[]{:S(2)}, u32[]{:S(2)}) %collective-permute-start.34) | collective-permute-done | bytes 163872 | tf_op jit(solution)/shard_map/ppermute | solution.py:235
  138.5 4.2 %collective-permute-done.75.refs_1_ = bf16[32,2560]{1,0:T(8,128)(2,1)S(1)} collective-permute-done((bf16[32,2560]{1,0:T(8,128)(2,1)S(1)}, bf16[32,2560]{1,0:T(8,128)(2,1)S(1)}, u32[]{:S(2)}, u32[]{:S(2)}) %collective-permute-start.75) | collective-permute-done | bytes 163872 | tf_op jit(solution)/shard_map/ppermute | solution.py:235
  143.7 1.3 collective-permute-start.38
  145.1 117.5 %collective-permute-done.38.refs_2_ = bf16[32,2560]{1,0:T(8,128)(2,1)S(1)} collective-permute-done((bf16[32,2560]{1,0:T(8,128)(2,1)S(1)}, bf16[32,2560]{1,0:T(8,128)(2,1)S(1)}, u32[]{:S(2)}, u32[]{:S(2)}) %collective-permute-start.38) | collective-permute-done | bytes 163872 | tf_op jit(solution)/shard_map/ppermute | solution.py:235
  262.6 4.6 %shard_map.65 = (f32[32,2560]{1,0:T(8,128)S(1)}, bf16[32,2560]{1,0:T(8,128)(2,1)S(1)}) custom-call(s32[14]{0:T(128)S(4)} %get-tuple-element.93.flag.refs_0_, bf16[64,2560]{1,0:T(8,128)(2,1)S(1)} %collective-permute-done.37.refs_0_, bf16[64,2560]{1,0:T(8,128)(2,1)S(1)} %get-tuple-element.128.refs_1_, ...), custom_call_target="tpu_custom_call" | custom-call | flops 838860800 | bytes 13107200 | tf_op jit(solution)/shard_map/pallas_call | solution.py:160
  267.3 1.3 collective-permute-start.78
  268.7 1.4 collective-permute-start.40
  271.4 3.9 %collective-permute-done.40.refs_1_ = bf16[32,2560]{1,0:T(8,128)(2,1)S(1)} collective-permute-done((bf16[32,2560]{1,0:T(8,128)(2,1)S(1)}, bf16[32,2560]{1,0:T(8,128)(2,1)S(1)}, u32[]{:S(2)}, u32[]{:S(2)}) %collective-permute-start.40) | collective-permute-done | bytes 163872 | tf_op jit(solution)/shard_map/ppermute | solution.py:235
  275.6 2.6 collective-permute-done.79.refs_2_
  279.3 4.6 %shard_map.86 = (f32[32,2560]{1,0:T(8,128)S(1)}, bf16[32,2560]{1,0:T(8,128)(2,1)S(1)}) custom-call(s32[14]{0:T(128)S(4)} %get-tuple-element.93.flag.refs_0_, bf16[64,2560]{1,0:T(8,128)(2,1)S(1)} %collective-permute-done.78.refs_0_, bf16[64,2560]{1,0:T(8,128)(2,1)S(1)} %get-tuple-element.172.refs_1_, ...), custom_call_target="tpu_custom_call" | custom-call | flops 838860800 | bytes 13107200 | tf_op jit(solution)/shard_map/pallas_call | solution.py:160
  284.0 1.4 collective-permute-done.80
  285.4 1.4 collective-permute-start.81
  286.9 4.9 %collective-permute-done.81.refs_1_ = bf16[32,2560]{1,0:T(8,128)(2,1)S(1)} collective-permute-done((bf16[32,2560]{1,0:T(8,128)(2,1)S(1)}, bf16[32,2560]{1,0:T(8,128)(2,1)S(1)}, u32[]{:S(2)}, u32[]{:S(2)}) %collective-permute-start.81) | collective-permute-done | bytes 163872 | tf_op jit(solution)/shard_map/ppermute | solution.py:235
  (210 shorter events, 57.5 us)
Async XLA Ops:
  1.3 9.2 %collective-permute-start = (bf16[1,16,2560]{2,1,0:T(8,128)(2,1)S(1)}, bf16[1,16,2560]{2,1,0:T(8,128)(2,1)S(1)}, u32[]{:S(2)}, u32[]{:S(2)}) collective-permute-start(bf16[1,16,2560]{2,1,0:T(8,128)(2,1)S(1)} %get-tuple-element.175), channel_id=1, source_target_pairs={{0,2},{1,3},{2,0},{3,1},{4,6},{5,7},{6,4},{7,5},{8,10},{9,11},{10,... | collective-permute-start | bytes 245768 | tf_op jit(solution)/shard_map/ppermute | solution.py:235
  15.4 8.8 %collective-permute-start.2 = (bf16[64,2560]{1,0:T(8,128)(2,1)S(1)}, bf16[64,2560]{1,0:T(8,128)(2,1)S(1)}, u32[]{:S(2)}, u32[]{:S(2)}) collective-permute-start(bf16[64,2560]{1,0:T(8,128)(2,1)S(1)} %get-tuple-element.100), channel_id=1, source_target_pairs={{0,4},{1,5},{2,6},{3,7}} | collective-permute-start | bytes 983048 | tf_op jit(solution)/shard_map/ppermute | solution.py:235
  16.7 7.5 %collective-permute-start.42 = (bf16[32,2560]{1,0:T(8,128)(2,1)S(1)}, bf16[32,2560]{1,0:T(8,128)(2,1)S(1)}, u32[]{:S(2)}, u32[]{:S(2)}) collective-permute-start(bf16[32,2560]{1,0:T(8,128)(2,1)S(1)} %bitcast.26), channel_id=1, source_target_pairs={{0,1},{1,0},{2,3},{3,2},{4,5},{5,4},{6,7},{7,6},{8,9},{9,8},{10,11... | collective-permute-start | bytes 491528 | tf_op jit(solution)/shard_map/ppermute | solution.py:235
  24.2 9.1 %collective-permute-start.3 = (bf16[32,2560]{1,0:T(8,128)(2,1)S(1)}, bf16[32,2560]{1,0:T(8,128)(2,1)S(1)}, u32[]{:S(2)}, u32[]{:S(2)}) collective-permute-start(bf16[32,2560]{1,0:T(8,128)(2,1)S(1)} %get-tuple-element.103), channel_id=1, source_target_pairs={{0,1},{1,0},{2,3},{3,2},{4,5},{5,4},{6,7},{7,6},{8,9},{9,8},{10,11... | collective-permute-start | bytes 491528 | tf_op jit(solution)/shard_map/ppermute | solution.py:235
  27.6 13.2 %collective-permute-start.43 = (bf16[64,2560]{1,0:T(8,128)(2,1)S(1)}, bf16[64,2560]{1,0:T(8,128)(2,1)S(1)}, u32[]{:S(2)}, u32[]{:S(2)}) collective-permute-start(bf16[64,2560]{1,0:T(8,128)(2,1)S(1)} %get-tuple-element.139), channel_id=1, source_target_pairs={{0,4},{1,5},{2,6},{3,7}} | collective-permute-start | bytes 983048 | tf_op jit(solution)/shard_map/ppermute | solution.py:235
  33.3 6.3 %collective-permute-start.4 = (bf16[32,2560]{1,0:T(8,128)(2,1)S(1)}, bf16[32,2560]{1,0:T(8,128)(2,1)S(1)}, u32[]{:S(2)}, u32[]{:S(2)}) collective-permute-start(bf16[32,2560]{1,0:T(8,128)(2,1)S(1)} %add_convert_fusion.13.refs_0_), channel_id=1, source_target_pairs={{0,2},{1,3},{2,0},{3,1},{4,6},{5,7},{6,4},{7,5},{8,10},{9,11},{10,... | collective-permute-start | bytes 491528 | tf_op jit(solution)/shard_map/ppermute | solution.py:235
  42.3 6.3 %collective-permute-start.45 = (bf16[32,2560]{1,0:T(8,128)(2,1)S(1)}, bf16[32,2560]{1,0:T(8,128)(2,1)S(1)}, u32[]{:S(2)}, u32[]{:S(2)}) collective-permute-start(bf16[32,2560]{1,0:T(8,128)(2,1)S(1)} %add_convert_fusion.6.refs_0_), channel_id=1, source_target_pairs={{0,2},{1,3},{2,0},{3,1},{4,6},{5,7},{6,4},{7,5},{8,10},{9,11},{10,... | collective-permute-start | bytes 491528 | tf_op jit(solution)/shard_map/ppermute | solution.py:235
  43.1 7.0 %collective-permute-start.7 = (bf16[64,2560]{1,0:T(8,128)(2,1)S(1)}, bf16[64,2560]{1,0:T(8,128)(2,1)S(1)}, u32[]{:S(2)}, u32[]{:S(2)}) collective-permute-start(bf16[64,2560]{1,0:T(8,128)(2,1)S(1)} %get-tuple-element.104), channel_id=1, source_target_pairs={{8,12},{9,13},{10,14},{11,15}} | collective-permute-start | bytes 983048 | tf_op jit(solution)/shard_map/ppermute | solution.py:235
  51.5 7.8 %collective-permute-start.48 = (bf16[64,2560]{1,0:T(8,128)(2,1)S(1)}, bf16[64,2560]{1,0:T(8,128)(2,1)S(1)}, u32[]{:S(2)}, u32[]{:S(2)}) collective-permute-start(bf16[64,2560]{1,0:T(8,128)(2,1)S(1)} %get-tuple-element.144), channel_id=1, source_target_pairs={{8,12},{9,13},{10,14},{11,15}} | collective-permute-start | bytes 983048 | tf_op jit(solution)/shard_map/ppermute | solution.py:235
  52.2 6.3 %collective-permute-start.10 = (bf16[32,2560]{1,0:T(8,128)(2,1)S(1)}, bf16[32,2560]{1,0:T(8,128)(2,1)S(1)}, u32[]{:S(2)}, u32[]{:S(2)}) collective-permute-start(bf16[32,2560]{1,0:T(8,128)(2,1)S(1)} %add_convert_fusion.12.refs_0_), channel_id=1, source_target_pairs={{0,2},{1,3},{2,0},{3,1},{4,6},{5,7},{6,4},{7,5},{8,10},{9,11},{10,... | collective-permute-start | bytes 491528 | tf_op jit(solution)/shard_map/ppermute | solution.py:235
  60.8 6.3 %collective-permute-start.51 = (bf16[32,2560]{1,0:T(8,128)(2,1)S(1)}, bf16[32,2560]{1,0:T(8,128)(2,1)S(1)}, u32[]{:S(2)}, u32[]{:S(2)}) collective-permute-start(bf16[32,2560]{1,0:T(8,128)(2,1)S(1)} %add_convert_fusion.5.refs_0_), channel_id=1, source_target_pairs={{0,2},{1,3},{2,0},{3,1},{4,6},{5,7},{6,4},{7,5},{8,10},{9,11},{10,... | collective-permute-start | bytes 491528 | tf_op jit(solution)/shard_map/ppermute | solution.py:235
  61.6 7.0 %collective-permute-start.13 = (bf16[64,2560]{1,0:T(8,128)(2,1)S(1)}, bf16[64,2560]{1,0:T(8,128)(2,1)S(1)}, u32[]{:S(2)}, u32[]{:S(2)}) collective-permute-start(bf16[64,2560]{1,0:T(8,128)(2,1)S(1)} %get-tuple-element.108), channel_id=1, source_target_pairs={{16,20},{17,21},{18,22},{19,23}} | collective-permute-start | bytes 983048 | tf_op jit(solution)/shard_map/ppermute | solution.py:235
  70.0 7.8 %collective-permute-start.54 = (bf16[64,2560]{1,0:T(8,128)(2,1)S(1)}, bf16[64,2560]{1,0:T(8,128)(2,1)S(1)}, u32[]{:S(2)}, u32[]{:S(2)}) collective-permute-start(bf16[64,2560]{1,0:T(8,128)(2,1)S(1)} %get-tuple-element.149), channel_id=1, source_target_pairs={{16,20},{17,21},{18,22},{19,23}} | collective-permute-start | bytes 983048 | tf_op jit(solution)/shard_map/ppermute | solution.py:235
  70.8 6.3 %collective-permute-start.16 = (bf16[32,2560]{1,0:T(8,128)(2,1)S(1)}, bf16[32,2560]{1,0:T(8,128)(2,1)S(1)}, u32[]{:S(2)}, u32[]{:S(2)}) collective-permute-start(bf16[32,2560]{1,0:T(8,128)(2,1)S(1)} %add_convert_fusion.11.refs_0_), channel_id=1, source_target_pairs={{0,2},{1,3},{2,0},{3,1},{4,6},{5,7},{6,4},{7,5},{8,10},{9,11},{10,... | collective-permute-start | bytes 491528 | tf_op jit(solution)/shard_map/ppermute | solution.py:235
  80.1 7.0 %collective-permute-start.20 = (bf16[32,2560]{1,0:T(8,128)(2,1)S(1)}, bf16[32,2560]{1,0:T(8,128)(2,1)S(1)}, u32[]{:S(2)}, u32[]{:S(2)}) collective-permute-start(bf16[32,2560]{1,0:T(8,128)(2,1)S(1)} %shard_map.54), channel_id=1, source_target_pairs={{20,28},{21,29},{22,30},{23,31}} | collective-permute-start | bytes 491528 | tf_op jit(solution)/shard_map/ppermute | solution.py:235
  80.8 6.4 %collective-permute-start.19 = (bf16[64,2560]{1,0:T(8,128)(2,1)S(1)}, bf16[64,2560]{1,0:T(8,128)(2,1)S(1)}, u32[]{:S(2)}, u32[]{:S(2)}) collective-permute-start(bf16[64,2560]{1,0:T(8,128)(2,1)S(1)} %get-tuple-element.112), channel_id=1, source_target_pairs={{24,28},{25,29},{26,30},{27,31},{28,24},{29,25},{30,26},{31,27}} | collective-permute-start | bytes 983048 | tf_op jit(solution)/shard_map/ppermute | solution.py:235
  88.7 8.2 %collective-permute-start.60 = (bf16[64,2560]{1,0:T(8,128)(2,1)S(1)}, bf16[64,2560]{1,0:T(8,128)(2,1)S(1)}, u32[]{:S(2)}, u32[]{:S(2)}) collective-permute-start(bf16[64,2560]{1,0:T(8,128)(2,1)S(1)} %get-tuple-element.154), channel_id=1, source_target_pairs={{24,28},{25,29},{26,30},{27,31},{28,24},{29,25},{30,26},{31,27}} | collective-permute-start | bytes 983048 | tf_op jit(solution)/shard_map/ppermute | solution.py:235
  89.6 6.3 %collective-permute-start.22 = (bf16[32,2560]{1,0:T(8,128)(2,1)S(1)}, bf16[32,2560]{1,0:T(8,128)(2,1)S(1)}, u32[]{:S(2)}, u32[]{:S(2)}) collective-permute-start(bf16[32,2560]{1,0:T(8,128)(2,1)S(1)} %add_convert_fusion.10.refs_1_), channel_id=1, source_target_pairs={{0,2},{1,3},{2,0},{3,1},{4,6},{5,7},{6,4},{7,5},{8,10},{9,11},{10,... | collective-permute-start | bytes 491528 | tf_op jit(solution)/shard_map/ppermute | solution.py:235
  98.4 6.3 %collective-permute-start.63 = (bf16[32,2560]{1,0:T(8,128)(2,1)S(1)}, bf16[32,2560]{1,0:T(8,128)(2,1)S(1)}, u32[]{:S(2)}, u32[]{:S(2)}) collective-permute-start(bf16[32,2560]{1,0:T(8,128)(2,1)S(1)} %add_convert_fusion.3.refs_1_), channel_id=1, source_target_pairs={{0,2},{1,3},{2,0},{3,1},{4,6},{5,7},{6,4},{7,5},{8,10},{9,11},{10,... | collective-permute-start | bytes 491528 | tf_op jit(solution)/shard_map/ppermute | solution.py:235
  99.2 7.3 %collective-permute-start.25 = (bf16[64,2560]{1,0:T(8,128)(2,1)S(1)}, bf16[64,2560]{1,0:T(8,128)(2,1)S(1)}, u32[]{:S(2)}, u32[]{:S(2)}) collective-permute-start(bf16[64,2560]{1,0:T(8,128)(2,1)S(1)} %shard_map.58), channel_id=1, source_target_pairs={{20,16},{21,17},{22,18},{23,19}} | collective-permute-start | bytes 983048 | tf_op jit(solution)/shard_map/ppermute | solution.py:235
  107.9 8.0 %collective-permute-start.66 = (bf16[64,2560]{1,0:T(8,128)(2,1)S(1)}, bf16[64,2560]{1,0:T(8,128)(2,1)S(1)}, u32[]{:S(2)}, u32[]{:S(2)}) collective-permute-start(bf16[64,2560]{1,0:T(8,128)(2,1)S(1)} %shard_map.79), channel_id=1, source_target_pairs={{20,16},{21,17},{22,18},{23,19}} | collective-permute-start | bytes 983048 | tf_op jit(solution)/shard_map/ppermute | solution.py:235
  108.6 6.3 %collective-permute-start.28 = (bf16[32,2560]{1,0:T(8,128)(2,1)S(1)}, bf16[32,2560]{1,0:T(8,128)(2,1)S(1)}, u32[]{:S(2)}, u32[]{:S(2)}) collective-permute-start(bf16[32,2560]{1,0:T(8,128)(2,1)S(1)} %add_convert_fusion.9.refs_0_), channel_id=1, source_target_pairs={{0,2},{1,3},{2,0},{3,1},{4,6},{5,7},{6,4},{7,5},{8,10},{9,11},{10,... | collective-permute-start | bytes 491528 | tf_op jit(solution)/shard_map/ppermute | solution.py:235
  109.4 6.5 %collective-permute-start.67 = (bf16[32,2560]{1,0:T(8,128)(2,1)S(1)}, bf16[32,2560]{1,0:T(8,128)(2,1)S(1)}, u32[]{:S(2)}, u32[]{:S(2)}) collective-permute-start(bf16[32,2560]{1,0:T(8,128)(2,1)S(1)} %shard_map.78), channel_id=1, source_target_pairs={{24,16},{25,17},{26,18},{27,19}} | collective-permute-start | bytes 491528 | tf_op jit(solution)/shard_map/ppermute | solution.py:235
  118.2 7.3 %collective-permute-start.31 = (bf16[64,2560]{1,0:T(8,128)(2,1)S(1)}, bf16[64,2560]{1,0:T(8,128)(2,1)S(1)}, u32[]{:S(2)}, u32[]{:S(2)}) collective-permute-start(bf16[64,2560]{1,0:T(8,128)(2,1)S(1)} %shard_map.61), channel_id=1, source_target_pairs={{12,8},{13,9},{14,10},{15,11}} | collective-permute-start | bytes 983048 | tf_op jit(solution)/shard_map/ppermute | solution.py:235
  126.9 8.0 %collective-permute-start.72 = (bf16[64,2560]{1,0:T(8,128)(2,1)S(1)}, bf16[64,2560]{1,0:T(8,128)(2,1)S(1)}, u32[]{:S(2)}, u32[]{:S(2)}) collective-permute-start(bf16[64,2560]{1,0:T(8,128)(2,1)S(1)} %shard_map.82), channel_id=1, source_target_pairs={{12,8},{13,9},{14,10},{15,11}} | collective-permute-start | bytes 983048 | tf_op jit(solution)/shard_map/ppermute | solution.py:235
  128.4 6.5 %collective-permute-start.73 = (bf16[32,2560]{1,0:T(8,128)(2,1)S(1)}, bf16[32,2560]{1,0:T(8,128)(2,1)S(1)}, u32[]{:S(2)}, u32[]{:S(2)}) collective-permute-start(bf16[32,2560]{1,0:T(8,128)(2,1)S(1)} %shard_map.81), channel_id=1, source_target_pairs={{16,8},{17,9},{18,10},{19,11}} | collective-permute-start | bytes 491528 | tf_op jit(solution)/shard_map/ppermute | solution.py:235
  137.2 125.4 %collective-permute-start.37 = (bf16[64,2560]{1,0:T(8,128)(2,1)S(1)}, bf16[64,2560]{1,0:T(8,128)(2,1)S(1)}, u32[]{:S(2)}, u32[]{:S(2)}) collective-permute-start(bf16[64,2560]{1,0:T(8,128)(2,1)S(1)} %shard_map.64), channel_id=1, source_target_pairs={{4,0},{5,1},{6,2},{7,3}} | collective-permute-start | bytes 983048 | tf_op jit(solution)/shard_map/ppermute | solution.py:235
  143.7 118.9 %collective-permute-start.38 = (bf16[32,2560]{1,0:T(8,128)(2,1)S(1)}, bf16[32,2560]{1,0:T(8,128)(2,1)S(1)}, u32[]{:S(2)}, u32[]{:S(2)}) collective-permute-start(bf16[32,2560]{1,0:T(8,128)(2,1)S(1)} %shard_map.63), channel_id=1, source_target_pairs={{8,0},{9,1},{10,2},{11,3}} | collective-permute-start | bytes 491528 | tf_op jit(solution)/shard_map/ppermute | solution.py:235
  145.0 122.3 %collective-permute-start.77 = (bf16[32,2560]{1,0:T(8,128)(2,1)S(1)}, bf16[32,2560]{1,0:T(8,128)(2,1)S(1)}, u32[]{:S(2)}, u32[]{:S(2)}) collective-permute-start(bf16[32,2560]{1,0:T(8,128)(2,1)S(1)} %collective-permute-done.76.refs_0_), channel_id=1, source_target_pairs={{0,1},{1,0},{2,3},{3,2},{4,5},{5,4},{6,7},{7,6},{8,9},{9,8},{10,11... | collective-permute-start | bytes 491528 | tf_op jit(solution)/shard_map/ppermute | solution.py:235
  267.3 12.0 %collective-permute-start.78 = (bf16[64,2560]{1,0:T(8,128)(2,1)S(1)}, bf16[64,2560]{1,0:T(8,128)(2,1)S(1)}, u32[]{:S(2)}, u32[]{:S(2)}) collective-permute-start(bf16[64,2560]{1,0:T(8,128)(2,1)S(1)} %shard_map.85), channel_id=1, source_target_pairs={{4,0},{5,1},{6,2},{7,3}} | collective-permute-start | bytes 983048 | tf_op jit(solution)/shard_map/ppermute | solution.py:235
  268.7 6.6 %collective-permute-start.40 = (bf16[32,2560]{1,0:T(8,128)(2,1)S(1)}, bf16[32,2560]{1,0:T(8,128)(2,1)S(1)}, u32[]{:S(2)}, u32[]{:S(2)}) collective-permute-start(bf16[32,2560]{1,0:T(8,128)(2,1)S(1)} %add_convert_fusion.7.refs_0_), channel_id=1, source_target_pairs={{0,2},{1,3},{2,0},{3,1},{4,6},{5,7},{6,4},{7,5},{8,10},{9,11},{10,... | collective-permute-start | bytes 491528 | tf_op jit(solution)/shard_map/ppermute | solution.py:235
  270.1 8.1 %collective-permute-start.79 = (bf16[32,2560]{1,0:T(8,128)(2,1)S(1)}, bf16[32,2560]{1,0:T(8,128)(2,1)S(1)}, u32[]{:S(2)}, u32[]{:S(2)}) collective-permute-start(bf16[32,2560]{1,0:T(8,128)(2,1)S(1)} %shard_map.84), channel_id=1, source_target_pairs={{8,0},{9,1},{10,2},{11,3}} | collective-permute-start | bytes 491528 | tf_op jit(solution)/shard_map/ppermute | solution.py:235
  (52 other events, 120.8 us)

commit v3 on v2

--- a/solution.py
+++ b/solution.py
@@ -158,7 +158,7 @@
     D = w.shape[0]
     args = (flag, arrived, w) if mode == "fwd" else (flag, arrived, slope, w)
     return pl.pallas_call(
-        functools.partial(second_kernel, mode, at, tile_of(D)),
+        functools.partial(second_kernel, mode, at, D // 2 if D % 256 == 0 else tile_of(D)),
         in_specs=[SMEM] + [VMEM] * (len(args) - 1),
         out_specs=[VMEM] * 2,
         out_shape=[
@@ -272,7 +272,7 @@
         return x.reshape(h, D)
 
     everyone = [(s, s) for s in range(S)]
-    w, roles = load_weights(w, roles)
+    w, roles = load_weights(pltpu.with_memory_space_constraint(w, pltpu.HBM), roles)
     seed = [spread(own[0], everyone, roles)] + [None] * (B - 1)
     main = list(seed)
     rest = list(seed)
@@ -340,9 +340,7 @@
                 saved[b][j] if backward else None, gain,
             )
             gate = fresh
-            piece = lax.dynamic_index_in_dim(
-                fresh.reshape(hi, share, D), high, 0, keepdims=False
-            )
+            piece = lax.dynamic_index_in_dim(fresh.reshape(hi, share, D), high, 0, keepdims=False)
             results[b] = jnp.where(oks[t], piece, results[b])
             if t < top:
                 if b > 0:

time: 294 us -> 288 us (0.980)
  local copies, waits for them, and re-layouts: 4.86 us -> 0.14 us
  Pallas kernels: 20.3 us -> 23.6 us
  waiting for transfers between devices: 208 us -> 205 us
    unnamed x5 -> x3, local copies, waits for them, and re-layouts: 4.75 us -> 0.02 us
    pallas_call x1, Pallas kernels: 1.43 us -> 5.27 us  [load_weights(): pl.pallas_call(kernel, in_specs=[HBM, SMEM], out_specs=[VMEM, SMEM], out_...]
    ppermute x82, waiting for transfers between devices: 208 us -> 205 us  [send(): return lax.ppermute(x, AXES, route)]
  transfers between devices with their start and end apart: 82 -> 82, of which waited for: 33 -> 33; matrix products, arithmetic and copies ran while one was open for 0% -> 0% of each run, Pallas kernels for 5% -> 7%
where the time goes in v3:
time: 288 us
  waiting for transfers between devices  205 us (71%)
  starting transfers between devices  55.1 us (19%)
  Pallas kernels  23.6 us (8%)
  other arithmetic  2.97 us (1%)
    ppermute x82, waiting for transfers between devices, send(): return lax.ppermute(x, AXES, route)  205 us
    ppermute x82, starting transfers between devices, send(): return lax.ppermute(x, AXES, route)  55.1 us
    pallas_call x14, Pallas kernels, second(): pl.pallas_call(functools.partial(second_kernel, mode, at, D // 2 if D % 2...  8.6 us
    pallas_call x14, Pallas kernels, first(): pl.pallas_call(functools.partial(first_kernel, mode, at, tile_of(F)), in_...  6.96 us
  transfers between devices with their start and end apart: 82, of which 33 were waited for; matrix products, arithmetic and copies ran while one was open for 0% of the time, Pallas kernels for 7%

profile of v3, /device:TPU:0, one launch (start us, length us, event | category | flops | bytes accessed | tf_op | source)
XLA Modules:
  0.0 287.7 jit_solution(7554914574533343102)
XLA Ops:
  1.3 3.1 %collective-permute-start = (bf16[1,16,2560]{2,1,0:T(8,128)(2,1)S(1)}, bf16[1,16,2560]{2,1,0:T(8,128)(2,1)S(1)}, u32[]{:S(2)}, u32[]{:S(2)}) collective-permute-start(bf16[1,16,2560]{2,1,0:T(8,128)(2,1)S(1)} %get-tuple-element.175), channel_id=1, source_target_pairs={{0,2},{1,3},{2,0},{3,1},{4,6},{5,7},{6,4},{7,5},{8,10},{9,11},{10,... | collective-permute-start | bytes 245768 | tf_op jit(solution)/shard_map/ppermute | solution.py:235
  4.3 5.3 %load_weights.1 = (bf16[2560,2560]{1,0:T(8,128)(2,1)S(1)}, s32[14]{0:T(128)S(4)}) custom-call(bf16[2560,2560]{1,0:T(8,128)(2,1)} %bitcast.47, s32[14]{0:T(128)S(1)} %pad_add_fusion.given), custom_call_target="tpu_custom_call" | custom-call | tf_op jit(solution)/shard_map/load_weights/pallas_call | solution.py:52
  9.8 1.3 collective-permute-done.1.refs_1_
  11.1 3.4 %shard_map.46 = (bf16[64,2560]{1,0:T(8,128)(2,1)S(1)}, bf16[64,2560]{1,0:T(8,128)(2,1)S(1)}) custom-call(s32[14]{0:T(128)S(4)} %get-tuple-element.93.flag.refs_0_, bf16[32,2560]{1,0:T(8,128)(2,1)S(1)} %bitcast.30, bf16[32,2560]{1,0:T(8,128)(2,1)S(1)} %collective-permute-done.1.refs_1_, f32[1,2560]{1,0:T(1,128)S(1)} %constant_dynamic-slice_fusion.refs_2_.refs_5_.refs_4_, ...), custom_call_target="tpu_custom_call" | custom-call | flops 838860800 | bytes 13107200 | tf_op jit(solution)/shard_map/pallas_call | solution.py:110
  14.5 1.3 collective-permute-start.2
  16.1 7.3 %collective-permute-done.2.refs_0_ = bf16[64,2560]{1,0:T(8,128)(2,1)S(1)} collective-permute-done((bf16[64,2560]{1,0:T(8,128)(2,1)S(1)}, bf16[64,2560]{1,0:T(8,128)(2,1)S(1)}, u32[]{:S(2)}, u32[]{:S(2)}) %collective-permute-start.2) | collective-permute-done | bytes 327712 | tf_op jit(solution)/shard_map/ppermute | solution.py:235
  23.3 3.4 %shard_map.67 = (bf16[64,2560]{1,0:T(8,128)(2,1)S(1)}, bf16[64,2560]{1,0:T(8,128)(2,1)S(1)}) custom-call(s32[14]{0:T(128)S(4)} %get-tuple-element.93.flag.refs_0_, bf16[32,2560]{1,0:T(8,128)(2,1)S(1)} %bitcast.26, bf16[32,2560]{1,0:T(8,128)(2,1)S(1)} %collective-permute-done.42.refs_1_, f32[1,2560]{1,0:T(1,128)S(1)} %constant_dynamic-slice_fusion.refs_2_.refs_5_.refs_4_, ...), custom_call_target="tpu_custom_call" | custom-call | flops 838860800 | bytes 13107200 | tf_op jit(solution)/shard_map/pallas_call | solution.py:110
  26.7 5.3 %collective-permute-start.43 = (bf16[64,2560]{1,0:T(8,128)(2,1)S(1)}, bf16[64,2560]{1,0:T(8,128)(2,1)S(1)}, u32[]{:S(2)}, u32[]{:S(2)}) collective-permute-start(bf16[64,2560]{1,0:T(8,128)(2,1)S(1)} %get-tuple-element.139), channel_id=1, source_target_pairs={{0,4},{1,5},{2,6},{3,7}} | collective-permute-start | bytes 983048 | tf_op jit(solution)/shard_map/ppermute | solution.py:235
  32.9 5.6 %collective-permute-done.4.refs_1_ = bf16[32,2560]{1,0:T(8,128)(2,1)S(1)} collective-permute-done((bf16[32,2560]{1,0:T(8,128)(2,1)S(1)}, bf16[32,2560]{1,0:T(8,128)(2,1)S(1)}, u32[]{:S(2)}, u32[]{:S(2)}) %collective-permute-start.4) | collective-permute-done | bytes 163872 | tf_op jit(solution)/shard_map/ppermute | solution.py:235
  42.5 4.8 %collective-permute-done.45.refs_1_ = bf16[32,2560]{1,0:T(8,128)(2,1)S(1)} collective-permute-done((bf16[32,2560]{1,0:T(8,128)(2,1)S(1)}, bf16[32,2560]{1,0:T(8,128)(2,1)S(1)}, u32[]{:S(2)}, u32[]{:S(2)}) %collective-permute-start.45) | collective-permute-done | bytes 163872 | tf_op jit(solution)/shard_map/ppermute | solution.py:235
  52.4 4.9 %collective-permute-done.10.refs_1_ = bf16[32,2560]{1,0:T(8,128)(2,1)S(1)} collective-permute-done((bf16[32,2560]{1,0:T(8,128)(2,1)S(1)}, bf16[32,2560]{1,0:T(8,128)(2,1)S(1)}, u32[]{:S(2)}, u32[]{:S(2)}) %collective-permute-start.10) | collective-permute-done | bytes 163872 | tf_op jit(solution)/shard_map/ppermute | solution.py:235
  61.0 4.8 %collective-permute-done.51.refs_1_ = bf16[32,2560]{1,0:T(8,128)(2,1)S(1)} collective-permute-done((bf16[32,2560]{1,0:T(8,128)(2,1)S(1)}, bf16[32,2560]{1,0:T(8,128)(2,1)S(1)}, u32[]{:S(2)}, u32[]{:S(2)}) %collective-permute-start.51) | collective-permute-done | bytes 163872 | tf_op jit(solution)/shard_map/ppermute | solution.py:235
  71.0 4.9 %collective-permute-done.16.refs_1_ = bf16[32,2560]{1,0:T(8,128)(2,1)S(1)} collective-permute-done((bf16[32,2560]{1,0:T(8,128)(2,1)S(1)}, bf16[32,2560]{1,0:T(8,128)(2,1)S(1)}, u32[]{:S(2)}, u32[]{:S(2)}) %collective-permute-start.16) | collective-permute-done | bytes 163872 | tf_op jit(solution)/shard_map/ppermute | solution.py:235
  80.5 4.0 %collective-permute-done.57.refs_1_ = bf16[32,2560]{1,0:T(8,128)(2,1)S(1)} collective-permute-done((bf16[32,2560]{1,0:T(8,128)(2,1)S(1)}, bf16[32,2560]{1,0:T(8,128)(2,1)S(1)}, u32[]{:S(2)}, u32[]{:S(2)}) %collective-permute-start.57) | collective-permute-done | bytes 163872 | tf_op jit(solution)/shard_map/ppermute | solution.py:235
  89.0 5.5 %collective-permute-done.22.refs_2_ = bf16[32,2560]{1,0:T(8,128)(2,1)S(1)} collective-permute-done((bf16[32,2560]{1,0:T(8,128)(2,1)S(1)}, bf16[32,2560]{1,0:T(8,128)(2,1)S(1)}, u32[]{:S(2)}, u32[]{:S(2)}) %collective-permute-start.22) | collective-permute-done | bytes 163872 | tf_op jit(solution)/shard_map/ppermute | solution.py:235
  98.5 4.8 %collective-permute-done.63.refs_2_ = bf16[32,2560]{1,0:T(8,128)(2,1)S(1)} collective-permute-done((bf16[32,2560]{1,0:T(8,128)(2,1)S(1)}, bf16[32,2560]{1,0:T(8,128)(2,1)S(1)}, u32[]{:S(2)}, u32[]{:S(2)}) %collective-permute-start.63) | collective-permute-done | bytes 163872 | tf_op jit(solution)/shard_map/ppermute | solution.py:235
  108.6 4.9 %collective-permute-done.28.refs_1_ = bf16[32,2560]{1,0:T(8,128)(2,1)S(1)} collective-permute-done((bf16[32,2560]{1,0:T(8,128)(2,1)S(1)}, bf16[32,2560]{1,0:T(8,128)(2,1)S(1)}, u32[]{:S(2)}, u32[]{:S(2)}) %collective-permute-start.28) | collective-permute-done | bytes 163872 | tf_op jit(solution)/shard_map/ppermute | solution.py:235
  117.5 4.8 %collective-permute-done.69.refs_1_ = bf16[32,2560]{1,0:T(8,128)(2,1)S(1)} collective-permute-done((bf16[32,2560]{1,0:T(8,128)(2,1)S(1)}, bf16[32,2560]{1,0:T(8,128)(2,1)S(1)}, u32[]{:S(2)}, u32[]{:S(2)}) %collective-permute-start.69) | collective-permute-done | bytes 163872 | tf_op jit(solution)/shard_map/ppermute | solution.py:235
  127.6 4.9 %collective-permute-done.34.refs_1_ = bf16[32,2560]{1,0:T(8,128)(2,1)S(1)} collective-permute-done((bf16[32,2560]{1,0:T(8,128)(2,1)S(1)}, bf16[32,2560]{1,0:T(8,128)(2,1)S(1)}, u32[]{:S(2)}, u32[]{:S(2)}) %collective-permute-start.34) | collective-permute-done | bytes 163872 | tf_op jit(solution)/shard_map/ppermute | solution.py:235
  135.8 1.3 collective-permute-start.37
  137.1 4.2 %collective-permute-done.75.refs_1_ = bf16[32,2560]{1,0:T(8,128)(2,1)S(1)} collective-permute-done((bf16[32,2560]{1,0:T(8,128)(2,1)S(1)}, bf16[32,2560]{1,0:T(8,128)(2,1)S(1)}, u32[]{:S(2)}, u32[]{:S(2)}) %collective-permute-start.75) | collective-permute-done | bytes 163872 | tf_op jit(solution)/shard_map/ppermute | solution.py:235
  142.3 1.3 collective-permute-start.38
  143.6 114.3 %collective-permute-done.38.refs_2_ = bf16[32,2560]{1,0:T(8,128)(2,1)S(1)} collective-permute-done((bf16[32,2560]{1,0:T(8,128)(2,1)S(1)}, bf16[32,2560]{1,0:T(8,128)(2,1)S(1)}, u32[]{:S(2)}, u32[]{:S(2)}) %collective-permute-start.38) | collective-permute-done | bytes 163872 | tf_op jit(solution)/shard_map/ppermute | solution.py:235
  257.9 4.2 %shard_map.65 = (f32[32,2560]{1,0:T(8,128)S(1)}, bf16[32,2560]{1,0:T(8,128)(2,1)S(1)}) custom-call(s32[14]{0:T(128)S(4)} %get-tuple-element.93.flag.refs_0_, bf16[64,2560]{1,0:T(8,128)(2,1)S(1)} %collective-permute-done.37.refs_0_, bf16[64,2560]{1,0:T(8,128)(2,1)S(1)} %get-tuple-element.128.refs_1_, ...), custom_call_target="tpu_custom_call" | custom-call | flops 838860800 | bytes 13107200 | tf_op jit(solution)/shard_map/pallas_call | solution.py:160
  262.3 1.3 collective-permute-start.78
  263.7 1.4 collective-permute-start.40
  266.3 3.9 %collective-permute-done.40.refs_1_ = bf16[32,2560]{1,0:T(8,128)(2,1)S(1)} collective-permute-done((bf16[32,2560]{1,0:T(8,128)(2,1)S(1)}, bf16[32,2560]{1,0:T(8,128)(2,1)S(1)}, u32[]{:S(2)}, u32[]{:S(2)}) %collective-permute-start.40) | collective-permute-done | bytes 163872 | tf_op jit(solution)/shard_map/ppermute | solution.py:235
  270.6 2.6 collective-permute-done.79.refs_2_
  274.3 4.2 %shard_map.86 = (f32[32,2560]{1,0:T(8,128)S(1)}, bf16[32,2560]{1,0:T(8,128)(2,1)S(1)}) custom-call(s32[14]{0:T(128)S(4)} %get-tuple-element.93.flag.refs_0_, bf16[64,2560]{1,0:T(8,128)(2,1)S(1)} %collective-permute-done.78.refs_0_, bf16[64,2560]{1,0:T(8,128)(2,1)S(1)} %get-tuple-element.172.refs_1_, ...), custom_call_target="tpu_custom_call" | custom-call | flops 838860800 | bytes 13107200 | tf_op jit(solution)/shard_map/pallas_call | solution.py:160
  278.6 1.4 collective-permute-done.80
  280.0 1.4 collective-permute-start.81
  281.5 4.9 %collective-permute-done.81.refs_1_ = bf16[32,2560]{1,0:T(8,128)(2,1)S(1)} collective-permute-done((bf16[32,2560]{1,0:T(8,128)(2,1)S(1)}, bf16[32,2560]{1,0:T(8,128)(2,1)S(1)}, u32[]{:S(2)}, u32[]{:S(2)}) %collective-permute-start.81) | collective-permute-done | bytes 163872 | tf_op jit(solution)/shard_map/ppermute | solution.py:235
  (208 shorter events, 56.2 us)
Async XLA Ops:
  1.3 8.4 %collective-permute-start = (bf16[1,16,2560]{2,1,0:T(8,128)(2,1)S(1)}, bf16[1,16,2560]{2,1,0:T(8,128)(2,1)S(1)}, u32[]{:S(2)}, u32[]{:S(2)}) collective-permute-start(bf16[1,16,2560]{2,1,0:T(8,128)(2,1)S(1)} %get-tuple-element.175), channel_id=1, source_target_pairs={{0,2},{1,3},{2,0},{3,1},{4,6},{5,7},{6,4},{7,5},{8,10},{9,11},{10,... | collective-permute-start | bytes 245768 | tf_op jit(solution)/shard_map/ppermute | solution.py:235
  14.5 8.8 %collective-permute-start.2 = (bf16[64,2560]{1,0:T(8,128)(2,1)S(1)}, bf16[64,2560]{1,0:T(8,128)(2,1)S(1)}, u32[]{:S(2)}, u32[]{:S(2)}) collective-permute-start(bf16[64,2560]{1,0:T(8,128)(2,1)S(1)} %get-tuple-element.100), channel_id=1, source_target_pairs={{0,4},{1,5},{2,6},{3,7}} | collective-permute-start | bytes 983048 | tf_op jit(solution)/shard_map/ppermute | solution.py:235
  15.9 7.5 %collective-permute-start.42 = (bf16[32,2560]{1,0:T(8,128)(2,1)S(1)}, bf16[32,2560]{1,0:T(8,128)(2,1)S(1)}, u32[]{:S(2)}, u32[]{:S(2)}) collective-permute-start(bf16[32,2560]{1,0:T(8,128)(2,1)S(1)} %bitcast.25), channel_id=1, source_target_pairs={{0,1},{1,0},{2,3},{3,2},{4,5},{5,4},{6,7},{7,6},{8,9},{9,8},{10,11... | collective-permute-start | bytes 491528 | tf_op jit(solution)/shard_map/ppermute | solution.py:235
  23.3 8.7 %collective-permute-start.3 = (bf16[32,2560]{1,0:T(8,128)(2,1)S(1)}, bf16[32,2560]{1,0:T(8,128)(2,1)S(1)}, u32[]{:S(2)}, u32[]{:S(2)}) collective-permute-start(bf16[32,2560]{1,0:T(8,128)(2,1)S(1)} %get-tuple-element.103), channel_id=1, source_target_pairs={{0,1},{1,0},{2,3},{3,2},{4,5},{5,4},{6,7},{7,6},{8,9},{9,8},{10,11... | collective-permute-start | bytes 491528 | tf_op jit(solution)/shard_map/ppermute | solution.py:235
  26.7 12.9 %collective-permute-start.43 = (bf16[64,2560]{1,0:T(8,128)(2,1)S(1)}, bf16[64,2560]{1,0:T(8,128)(2,1)S(1)}, u32[]{:S(2)}, u32[]{:S(2)}) collective-permute-start(bf16[64,2560]{1,0:T(8,128)(2,1)S(1)} %get-tuple-element.139), channel_id=1, source_target_pairs={{0,4},{1,5},{2,6},{3,7}} | collective-permute-start | bytes 983048 | tf_op jit(solution)/shard_map/ppermute | solution.py:235
  32.1 6.3 %collective-permute-start.4 = (bf16[32,2560]{1,0:T(8,128)(2,1)S(1)}, bf16[32,2560]{1,0:T(8,128)(2,1)S(1)}, u32[]{:S(2)}, u32[]{:S(2)}) collective-permute-start(bf16[32,2560]{1,0:T(8,128)(2,1)S(1)} %add_convert_fusion.13.refs_0_), channel_id=1, source_target_pairs={{0,2},{1,3},{2,0},{3,1},{4,6},{5,7},{6,4},{7,5},{8,10},{9,11},{10,... | collective-permute-start | bytes 491528 | tf_op jit(solution)/shard_map/ppermute | solution.py:235
  41.0 6.3 %collective-permute-start.45 = (bf16[32,2560]{1,0:T(8,128)(2,1)S(1)}, bf16[32,2560]{1,0:T(8,128)(2,1)S(1)}, u32[]{:S(2)}, u32[]{:S(2)}) collective-permute-start(bf16[32,2560]{1,0:T(8,128)(2,1)S(1)} %add_convert_fusion.6.refs_0_), channel_id=1, source_target_pairs={{0,2},{1,3},{2,0},{3,1},{4,6},{5,7},{6,4},{7,5},{8,10},{9,11},{10,... | collective-permute-start | bytes 491528 | tf_op jit(solution)/shard_map/ppermute | solution.py:235
  41.8 7.0 %collective-permute-start.7 = (bf16[64,2560]{1,0:T(8,128)(2,1)S(1)}, bf16[64,2560]{1,0:T(8,128)(2,1)S(1)}, u32[]{:S(2)}, u32[]{:S(2)}) collective-permute-start(bf16[64,2560]{1,0:T(8,128)(2,1)S(1)} %get-tuple-element.104), channel_id=1, source_target_pairs={{8,12},{9,13},{10,14},{11,15}} | collective-permute-start | bytes 983048 | tf_op jit(solution)/shard_map/ppermute | solution.py:235
  50.2 7.8 %collective-permute-start.48 = (bf16[64,2560]{1,0:T(8,128)(2,1)S(1)}, bf16[64,2560]{1,0:T(8,128)(2,1)S(1)}, u32[]{:S(2)}, u32[]{:S(2)}) collective-permute-start(bf16[64,2560]{1,0:T(8,128)(2,1)S(1)} %get-tuple-element.144), channel_id=1, source_target_pairs={{8,12},{9,13},{10,14},{11,15}} | collective-permute-start | bytes 983048 | tf_op jit(solution)/shard_map/ppermute | solution.py:235
  51.0 6.3 %collective-permute-start.10 = (bf16[32,2560]{1,0:T(8,128)(2,1)S(1)}, bf16[32,2560]{1,0:T(8,128)(2,1)S(1)}, u32[]{:S(2)}, u32[]{:S(2)}) collective-permute-start(bf16[32,2560]{1,0:T(8,128)(2,1)S(1)} %add_convert_fusion.12.refs_0_), channel_id=1, source_target_pairs={{0,2},{1,3},{2,0},{3,1},{4,6},{5,7},{6,4},{7,5},{8,10},{9,11},{10,... | collective-permute-start | bytes 491528 | tf_op jit(solution)/shard_map/ppermute | solution.py:235
  59.6 6.3 %collective-permute-start.51 = (bf16[32,2560]{1,0:T(8,128)(2,1)S(1)}, bf16[32,2560]{1,0:T(8,128)(2,1)S(1)}, u32[]{:S(2)}, u32[]{:S(2)}) collective-permute-start(bf16[32,2560]{1,0:T(8,128)(2,1)S(1)} %add_convert_fusion.5.refs_0_), channel_id=1, source_target_pairs={{0,2},{1,3},{2,0},{3,1},{4,6},{5,7},{6,4},{7,5},{8,10},{9,11},{10,... | collective-permute-start | bytes 491528 | tf_op jit(solution)/shard_map/ppermute | solution.py:235
  60.3 7.0 %collective-permute-start.13 = (bf16[64,2560]{1,0:T(8,128)(2,1)S(1)}, bf16[64,2560]{1,0:T(8,128)(2,1)S(1)}, u32[]{:S(2)}, u32[]{:S(2)}) collective-permute-start(bf16[64,2560]{1,0:T(8,128)(2,1)S(1)} %get-tuple-element.108), channel_id=1, source_target_pairs={{16,20},{17,21},{18,22},{19,23}} | collective-permute-start | bytes 983048 | tf_op jit(solution)/shard_map/ppermute | solution.py:235
  68.8 7.8 %collective-permute-start.54 = (bf16[64,2560]{1,0:T(8,128)(2,1)S(1)}, bf16[64,2560]{1,0:T(8,128)(2,1)S(1)}, u32[]{:S(2)}, u32[]{:S(2)}) collective-permute-start(bf16[64,2560]{1,0:T(8,128)(2,1)S(1)} %get-tuple-element.149), channel_id=1, source_target_pairs={{16,20},{17,21},{18,22},{19,23}} | collective-permute-start | bytes 983048 | tf_op jit(solution)/shard_map/ppermute | solution.py:235
  69.5 6.3 %collective-permute-start.16 = (bf16[32,2560]{1,0:T(8,128)(2,1)S(1)}, bf16[32,2560]{1,0:T(8,128)(2,1)S(1)}, u32[]{:S(2)}, u32[]{:S(2)}) collective-permute-start(bf16[32,2560]{1,0:T(8,128)(2,1)S(1)} %add_convert_fusion.11.refs_0_), channel_id=1, source_target_pairs={{0,2},{1,3},{2,0},{3,1},{4,6},{5,7},{6,4},{7,5},{8,10},{9,11},{10,... | collective-permute-start | bytes 491528 | tf_op jit(solution)/shard_map/ppermute | solution.py:235
  78.1 6.3 %collective-permute-start.57 = (bf16[32,2560]{1,0:T(8,128)(2,1)S(1)}, bf16[32,2560]{1,0:T(8,128)(2,1)S(1)}, u32[]{:S(2)}, u32[]{:S(2)}) collective-permute-start(bf16[32,2560]{1,0:T(8,128)(2,1)S(1)} %add_convert_fusion.4.refs_0_), channel_id=1, source_target_pairs={{0,2},{1,3},{2,0},{3,1},{4,6},{5,7},{6,4},{7,5},{8,10},{9,11},{10,... | collective-permute-start | bytes 491528 | tf_op jit(solution)/shard_map/ppermute | solution.py:235
  78.9 7.0 %collective-permute-start.20 = (bf16[32,2560]{1,0:T(8,128)(2,1)S(1)}, bf16[32,2560]{1,0:T(8,128)(2,1)S(1)}, u32[]{:S(2)}, u32[]{:S(2)}) collective-permute-start(bf16[32,2560]{1,0:T(8,128)(2,1)S(1)} %shard_map.54), channel_id=1, source_target_pairs={{20,28},{21,29},{22,30},{23,31}} | collective-permute-start | bytes 491528 | tf_op jit(solution)/shard_map/ppermute | solution.py:235
  87.4 8.1 %collective-permute-start.60 = (bf16[64,2560]{1,0:T(8,128)(2,1)S(1)}, bf16[64,2560]{1,0:T(8,128)(2,1)S(1)}, u32[]{:S(2)}, u32[]{:S(2)}) collective-permute-start(bf16[64,2560]{1,0:T(8,128)(2,1)S(1)} %get-tuple-element.154), channel_id=1, source_target_pairs={{24,28},{25,29},{26,30},{27,31},{28,24},{29,25},{30,26},{31,27}} | collective-permute-start | bytes 983048 | tf_op jit(solution)/shard_map/ppermute | solution.py:235
  88.1 6.3 %collective-permute-start.22 = (bf16[32,2560]{1,0:T(8,128)(2,1)S(1)}, bf16[32,2560]{1,0:T(8,128)(2,1)S(1)}, u32[]{:S(2)}, u32[]{:S(2)}) collective-permute-start(bf16[32,2560]{1,0:T(8,128)(2,1)S(1)} %add_convert_fusion.10.refs_1_), channel_id=1, source_target_pairs={{0,2},{1,3},{2,0},{3,1},{4,6},{5,7},{6,4},{7,5},{8,10},{9,11},{10,... | collective-permute-start | bytes 491528 | tf_op jit(solution)/shard_map/ppermute | solution.py:235
  97.0 6.3 %collective-permute-start.63 = (bf16[32,2560]{1,0:T(8,128)(2,1)S(1)}, bf16[32,2560]{1,0:T(8,128)(2,1)S(1)}, u32[]{:S(2)}, u32[]{:S(2)}) collective-permute-start(bf16[32,2560]{1,0:T(8,128)(2,1)S(1)} %add_convert_fusion.3.refs_1_), channel_id=1, source_target_pairs={{0,2},{1,3},{2,0},{3,1},{4,6},{5,7},{6,4},{7,5},{8,10},{9,11},{10,... | collective-permute-start | bytes 491528 | tf_op jit(solution)/shard_map/ppermute | solution.py:235
  97.8 7.3 %collective-permute-start.25 = (bf16[64,2560]{1,0:T(8,128)(2,1)S(1)}, bf16[64,2560]{1,0:T(8,128)(2,1)S(1)}, u32[]{:S(2)}, u32[]{:S(2)}) collective-permute-start(bf16[64,2560]{1,0:T(8,128)(2,1)S(1)} %shard_map.58), channel_id=1, source_target_pairs={{20,16},{21,17},{22,18},{23,19}} | collective-permute-start | bytes 983048 | tf_op jit(solution)/shard_map/ppermute | solution.py:235
  106.4 8.0 %collective-permute-start.66 = (bf16[64,2560]{1,0:T(8,128)(2,1)S(1)}, bf16[64,2560]{1,0:T(8,128)(2,1)S(1)}, u32[]{:S(2)}, u32[]{:S(2)}) collective-permute-start(bf16[64,2560]{1,0:T(8,128)(2,1)S(1)} %shard_map.79), channel_id=1, source_target_pairs={{20,16},{21,17},{22,18},{23,19}} | collective-permute-start | bytes 983048 | tf_op jit(solution)/shard_map/ppermute | solution.py:235
  107.2 6.3 %collective-permute-start.28 = (bf16[32,2560]{1,0:T(8,128)(2,1)S(1)}, bf16[32,2560]{1,0:T(8,128)(2,1)S(1)}, u32[]{:S(2)}, u32[]{:S(2)}) collective-permute-start(bf16[32,2560]{1,0:T(8,128)(2,1)S(1)} %add_convert_fusion.9.refs_0_), channel_id=1, source_target_pairs={{0,2},{1,3},{2,0},{3,1},{4,6},{5,7},{6,4},{7,5},{8,10},{9,11},{10,... | collective-permute-start | bytes 491528 | tf_op jit(solution)/shard_map/ppermute | solution.py:235
  108.0 6.5 %collective-permute-start.67 = (bf16[32,2560]{1,0:T(8,128)(2,1)S(1)}, bf16[32,2560]{1,0:T(8,128)(2,1)S(1)}, u32[]{:S(2)}, u32[]{:S(2)}) collective-permute-start(bf16[32,2560]{1,0:T(8,128)(2,1)S(1)} %shard_map.78), channel_id=1, source_target_pairs={{24,16},{25,17},{26,18},{27,19}} | collective-permute-start | bytes 491528 | tf_op jit(solution)/shard_map/ppermute | solution.py:235
  116.8 7.3 %collective-permute-start.31 = (bf16[64,2560]{1,0:T(8,128)(2,1)S(1)}, bf16[64,2560]{1,0:T(8,128)(2,1)S(1)}, u32[]{:S(2)}, u32[]{:S(2)}) collective-permute-start(bf16[64,2560]{1,0:T(8,128)(2,1)S(1)} %shard_map.61), channel_id=1, source_target_pairs={{12,8},{13,9},{14,10},{15,11}} | collective-permute-start | bytes 983048 | tf_op jit(solution)/shard_map/ppermute | solution.py:235
  125.4 8.0 %collective-permute-start.72 = (bf16[64,2560]{1,0:T(8,128)(2,1)S(1)}, bf16[64,2560]{1,0:T(8,128)(2,1)S(1)}, u32[]{:S(2)}, u32[]{:S(2)}) collective-permute-start(bf16[64,2560]{1,0:T(8,128)(2,1)S(1)} %shard_map.82), channel_id=1, source_target_pairs={{12,8},{13,9},{14,10},{15,11}} | collective-permute-start | bytes 983048 | tf_op jit(solution)/shard_map/ppermute | solution.py:235
  126.9 6.5 %collective-permute-start.73 = (bf16[32,2560]{1,0:T(8,128)(2,1)S(1)}, bf16[32,2560]{1,0:T(8,128)(2,1)S(1)}, u32[]{:S(2)}, u32[]{:S(2)}) collective-permute-start(bf16[32,2560]{1,0:T(8,128)(2,1)S(1)} %shard_map.81), channel_id=1, source_target_pairs={{16,8},{17,9},{18,10},{19,11}} | collective-permute-start | bytes 491528 | tf_op jit(solution)/shard_map/ppermute | solution.py:235
  135.8 122.1 %collective-permute-start.37 = (bf16[64,2560]{1,0:T(8,128)(2,1)S(1)}, bf16[64,2560]{1,0:T(8,128)(2,1)S(1)}, u32[]{:S(2)}, u32[]{:S(2)}) collective-permute-start(bf16[64,2560]{1,0:T(8,128)(2,1)S(1)} %shard_map.64), channel_id=1, source_target_pairs={{4,0},{5,1},{6,2},{7,3}} | collective-permute-start | bytes 983048 | tf_op jit(solution)/shard_map/ppermute | solution.py:235
  142.3 115.7 %collective-permute-start.38 = (bf16[32,2560]{1,0:T(8,128)(2,1)S(1)}, bf16[32,2560]{1,0:T(8,128)(2,1)S(1)}, u32[]{:S(2)}, u32[]{:S(2)}) collective-permute-start(bf16[32,2560]{1,0:T(8,128)(2,1)S(1)} %shard_map.63), channel_id=1, source_target_pairs={{8,0},{9,1},{10,2},{11,3}} | collective-permute-start | bytes 491528 | tf_op jit(solution)/shard_map/ppermute | solution.py:235
  143.6 118.7 %collective-permute-start.77 = (bf16[32,2560]{1,0:T(8,128)(2,1)S(1)}, bf16[32,2560]{1,0:T(8,128)(2,1)S(1)}, u32[]{:S(2)}, u32[]{:S(2)}) collective-permute-start(bf16[32,2560]{1,0:T(8,128)(2,1)S(1)} %collective-permute-done.76.refs_0_), channel_id=1, source_target_pairs={{0,1},{1,0},{2,3},{3,2},{4,5},{5,4},{6,7},{7,6},{8,9},{9,8},{10,11... | collective-permute-start | bytes 491528 | tf_op jit(solution)/shard_map/ppermute | solution.py:235
  262.3 12.0 %collective-permute-start.78 = (bf16[64,2560]{1,0:T(8,128)(2,1)S(1)}, bf16[64,2560]{1,0:T(8,128)(2,1)S(1)}, u32[]{:S(2)}, u32[]{:S(2)}) collective-permute-start(bf16[64,2560]{1,0:T(8,128)(2,1)S(1)} %shard_map.85), channel_id=1, source_target_pairs={{4,0},{5,1},{6,2},{7,3}} | collective-permute-start | bytes 983048 | tf_op jit(solution)/shard_map/ppermute | solution.py:235
  263.7 6.6 %collective-permute-start.40 = (bf16[32,2560]{1,0:T(8,128)(2,1)S(1)}, bf16[32,2560]{1,0:T(8,128)(2,1)S(1)}, u32[]{:S(2)}, u32[]{:S(2)}) collective-permute-start(bf16[32,2560]{1,0:T(8,128)(2,1)S(1)} %add_convert_fusion.7.refs_0_), channel_id=1, source_target_pairs={{0,2},{1,3},{2,0},{3,1},{4,6},{5,7},{6,4},{7,5},{8,10},{9,11},{10,... | collective-permute-start | bytes 491528 | tf_op jit(solution)/shard_map/ppermute | solution.py:235
  265.0 8.1 %collective-permute-start.79 = (bf16[32,2560]{1,0:T(8,128)(2,1)S(1)}, bf16[32,2560]{1,0:T(8,128)(2,1)S(1)}, u32[]{:S(2)}, u32[]{:S(2)}) collective-permute-start(bf16[32,2560]{1,0:T(8,128)(2,1)S(1)} %shard_map.84), channel_id=1, source_target_pairs={{8,0},{9,1},{10,2},{11,3}} | collective-permute-start | bytes 491528 | tf_op jit(solution)/shard_map/ppermute | solution.py:235
  (51 other events, 115.7 us)
